TPU v7x, 8 devices: a whole 2x2x1 slice. The times are simulated.
8 devices in a mesh: dp: 1 (over z), sp: 8 (over y, x, core).
Axes of the slice: x: 2, y: 2, z: 1, core: 2. Of those that a mesh axis runs over, the one named last changes fastest.
Arguments:
- image_tokens: bfloat16 [32, 1024, 1152], P('dp', 'sp')
- ln1_gain: float32 [2, 1152], replicated
- ln1_shift: float32 [2, 1152], replicated
- w_qkv: bfloat16 [2, 1152, 3, 16, 72], replicated
- b_qkv: float32 [2, 3, 16, 72], replicated
- w_out: bfloat16 [2, 16, 72, 1152], replicated
- b_out: float32 [2, 1152], replicated
- ln2_gain: float32 [2, 1152], replicated
- ln2_shift: float32 [2, 1152], replicated
- w_up: bfloat16 [2, 1152, 4304], replicated
- b_up: float32 [2, 4304], replicated
- w_down: bfloat16 [2, 4304, 1152], replicated
- b_down: float32 [2, 1152], replicated
Outputs:
- output: bfloat16 [32, 1024, 1152], P('dp', 'sp')
All inputs are finite; a program needn't handle non-finite values.
Results may differ from a plain program's by a relative error of at most 0.0143686.
Values are sent between devices in bfloat16 or wider.
A program may use at most 1 GiB of HBM per device.

v0:
```python
import jax
import jax.numpy as jnp
from jax import lax
from jax.sharding import PartitionSpec as P

LN_EPS = 1e-6


def layer_norm(tokens, ln_gain, ln_shift):
    values = tokens.astype(jnp.float32)
    mean_val = jnp.mean(values, axis=-1, keepdims=True)
    centred = values - mean_val
    var_val = jnp.mean(centred * centred, axis=-1, keepdims=True)
    return (centred * lax.rsqrt(var_val + LN_EPS) * ln_gain + ln_shift).astype(jnp.bfloat16)


def attend(q_part, k_part, v_part):
    score_scale = q_part.shape[-1] ** -0.5
    scores = jnp.einsum('bqhe,bkhe->bhqk', q_part, k_part, preferred_element_type=jnp.float32) * score_scale
    row_peak = jnp.max(scores, axis=-1, keepdims=True)
    prob_vals = jnp.exp(scores - row_peak)
    row_total = jnp.sum(prob_vals, axis=-1, keepdims=True)
    mixed_vals = jnp.einsum('bhqk,bkhe->bhqe', prob_vals.astype(jnp.bfloat16), v_part, preferred_element_type=jnp.float32)
    return (mixed_vals / row_total).astype(jnp.bfloat16)


def mlp_block(mid_state, ln2_gain, ln2_shift, w_up, b_up, w_down, b_down):
    normed = layer_norm(mid_state, ln2_gain, ln2_shift)
    up_proj = jnp.einsum('bsd,df->bsf', normed, w_up, preferred_element_type=jnp.float32) + b_up
    active = jax.nn.gelu(up_proj, approximate=True).astype(jnp.bfloat16)
    down_proj = jnp.einsum('bsf,fd->bsd', active, w_down, preferred_element_type=jnp.float32) + b_down
    return (mid_state.astype(jnp.float32) + down_proj).astype(jnp.bfloat16)


def solution(mesh):
    token_spec = P('dp', 'sp', None)

    def device_step(image_tokens, ln1_gain, ln1_shift, w_qkv, b_qkv, w_out, b_out, ln2_gain, ln2_shift, w_up, b_up, w_down, b_down):
        hidden = image_tokens
        for layer_idx in range(w_qkv.shape[0]):
            normed = layer_norm(hidden, ln1_gain[layer_idx], ln1_shift[layer_idx])
            qkv_local = (jnp.einsum('bsd,dthe->bsthe', normed, w_qkv[layer_idx], preferred_element_type=jnp.float32) + b_qkv[layer_idx]).astype(jnp.bfloat16)
            qkv_heads = lax.all_to_all(qkv_local, 'sp', 3, 1, tiled=True)
            attn_heads = attend(qkv_heads[:, :, 0], qkv_heads[:, :, 1], qkv_heads[:, :, 2])
            attn_tokens = lax.all_to_all(attn_heads, 'sp', 2, 1, tiled=True)
            attn_proj = jnp.einsum('bhse,hed->bsd', attn_tokens, w_out[layer_idx], preferred_element_type=jnp.float32) + b_out[layer_idx]
            mid_state = (hidden.astype(jnp.float32) + attn_proj).astype(jnp.bfloat16)
            hidden = mlp_block(mid_state, ln2_gain[layer_idx], ln2_shift[layer_idx], w_up[layer_idx], b_up[layer_idx], w_down[layer_idx], b_down[layer_idx])
        return hidden

    return jax.shard_map(device_step, mesh=mesh, in_specs=(token_spec,) + (P(),) * 12, out_specs=token_spec, check_vma=False)
```

profile of v0, /device:TPU:0, one launch (start us, length us, event | category | flops | bytes accessed | tf_op | source)
XLA Modules:
  0.0 2250.3 jit_solution(4084534086267112477)
XLA Ops:
  0.0 5.1 convert_reduce_fusion.3
  5.2 0.0 slice-start.2
  5.2 6.5 fusion.58
  11.6 0.0 copy-done.2
  11.7 0.6 slice_bitcast_fusion.12
  12.3 0.6 slice_reduce_fusion.6
  12.9 0.0 slice-done
  12.9 0.0 slice-done.2
  12.9 44.4 %add_convert_fusion.1 = bf16[32,128,3,16,72]{1,4,3,2,0:T(8,128)(2,1)} fusion(f32[3,16,72]{2,1,0:T(8,128)S(1)} %get-tuple-element.20, bf16[32,128,1152]{2,1,0:T(8,128)(2,1)S(1)} %bitcast.160, f32[1152]{0:T(1024)S(1)} %get-tuple-element.18, f32[1152]{0:T(1024)S(1)} %get-tuple-element.31, f32[32,128]{1,0:T(8,128)S(1)} %add_rsqrt_fusion.3, ...), kind=kOutput, calls=%fused_computation.29 | convolution fusion | flops 32671531008 | bytes 45767168 | tf_op jit(solution)/shard_map/bsd,dthe->bsthe/dot_general | solution.py:42
  57.4 19.5 copy.20
  76.9 317.6 %all_to_all.72 = bf16[32,128,3,16,72]{1,4,2,0,3:T(8,128)(2,1)} all-to-all(bf16[32,128,3,16,72]{1,4,2,0,3:T(8,128)(2,1)} %copy.20), channel_id=1, replica_groups=mesh['dp'=1,'sp'=8] {'sp'}, dimensions={3} | all-to-all | bytes 56623104 | tf_op jit(solution)/shard_map/all_to_all | solution.py:43
  394.5 19.7 copy.39
  414.2 41.8 %all_to_all.55 = bf16[32,1024,3,2,72]{1,4,3,0,2:T(8,128)(2,1)} reshape(bf16[32,8,128,3,2,72]{2,1,5,4,0,3:T(8,128)(2,1)} %bitcast.155) | data formatting | bytes 56623104 | tf_op jit(solution)/shard_map/all_to_all | solution.py:43
  456.0 92.9 %multiply_reduce_fusion.1 = (f32[32,2,1024]{2,1,0:T(2,128)S(1)}, f32[32,2,1024,1024]{2,3,1,0:T(8,128)}) fusion(bf16[32,1024,3,2,72]{1,4,3,0,2:T(8,128)(2,1)} %all_to_all.55), kind=kOutput, calls=%fused_computation.3 | convolution fusion | flops 9797828608 | bytes 287571968 | tf_op jit(solution)/shard_map/bqhe,bkhe->bhqk/dot_general | solution.py:19
  548.9 80.7 %fusion = f32[32,2,1024]{2,1,0:T(2,128)S(1)} fusion(f32[32,2,1024,1024]{2,3,1,0:T(8,128)} %get-tuple-element.22, f32[32,2,1024]{2,1,0:T(2,128)S(1)} %get-tuple-element.21), kind=kLoop, calls=%fused_computation.4 | loop fusion | flops 201261056 | bytes 268959744 | tf_op jit(solution)/shard_map/reduce_sum | solution.py:22
  629.6 87.4 %divide_convert_fusion.1 = bf16[32,2,1024,72]{2,3,1,0:T(8,128)(2,1)} fusion(f32[32,2,1024,1024]{2,3,1,0:T(8,128)} %get-tuple-element.22, f32[32,2,1024]{2,1,0:T(2,128)S(1)} %get-tuple-element.21, bf16[32,1024,3,2,72]{1,4,3,0,2:T(8,128)(2,1)} %all_to_all.55, f32[32,2,1024]{2,1,0:T(2,128)S(1)} %fusion), kind=kOutput, calls=%fused_computation.87 | convolution fusion | flops 9874440192 | bytes 287834112 | tf_op jit(solution)/shard_map/bhqk,bkhe->bhqe/dot_general | solution.py:23
  716.9 36.9 %copy.23 = bf16[32,2,1024,72]{3,1,0,2:T(2,128)(2,1)} copy(bf16[32,2,1024,72]{2,3,1,0:T(8,128)(2,1)} %divide_convert_fusion.1) | data formatting | bytes 18874368 | tf_op jit(solution)/shard_map/convert_element_type | solution.py:24
  753.8 0.0 copy-start.3
  753.9 4.8 all-to-all-start.1
  758.7 0.6 slice_reduce_fusion.5
  759.3 0.6 slice_reduce_fusion.4
  759.9 0.0 copy-done.10
  759.9 0.6 slice_reduce_fusion.2
  760.6 0.7 slice_reduce_fusion.1
  761.2 181.4 %all-to-all-done.1 = bf16[32,2,1024,72]{3,1,0,2:T(2,128)(2,1)} async-done(((bf16[32,2,1024,72]{3,1,0,2:T(2,128)(2,1)}), bf16[32,2,1024,72]{3,1,0,2:T(2,128)(2,1)}, u32[]{:S(2)}, u32[]{:S(2)}) %all-to-all-start.1) | async-done | bytes 9437216 | tf_op jit(solution)/shard_map/all_to_all | solution.py:45
  942.6 36.6 %copy.24 = bf16[32,2,8,128,72]{3,4,1,2,0:T(8,128)(2,1)} copy(bf16[32,2,8,128,72]{4,1,0,3,2:T(2,128)(2,1)} %bitcast.10) | data formatting | bytes 18874368 | tf_op jit(solution)/shard_map/all_to_all | solution.py:45
  979.2 19.9 convert_reduce_fusion.2
  999.1 0.0 copy-start.1
  999.2 2.8 fusion.54
  1001.9 72.5 %fusion.15.clone.7.clone.5 = bf16[32,128,4304]{1,2,0:T(8,128)(2,1)} fusion(f32[4304]{0:T(1024)S(1)} %get-tuple-element.5, bf16[32,128,1152]{2,1,0:T(8,128)(2,1)S(1)} %get-tuple-element.24, bf16[2,1152,4304]{1,2,0:T(8,128)(2,1)} %param.22, f32[1152]{0:T(1024)S(1)} %get-tuple-element.33, ...), kind=kOutput, calls=%fused_computation.19.clone.clone.clone.clone.clone.clone.clone.clone.clone.clone... | convolution fusion | flops 40822243328 | bytes 54671168 | tf_op jit(solution)/shard_map/bsd,df->bsf/dot_general | solution.py:29
  1074.5 55.1 %convert_reduce_fusion.1 = (f32[32,128]{1,0:T(8,128)S(1)}, bf16[32,128,1152]{2,1,0:T(8,128)(2,1)S(1)}) fusion(f32[1152]{0:T(1024)S(1)} %get-tuple-element.12, bf16[2,4304,1152]{2,1,0:T(8,128)(2,1)} %param.24, bf16[32,128,1152]{2,1,0:T(8,128)(2,1)} %copy-done.1, bf16[32,128,4304]{1,2,0:T(8,128)(2,1)} %fusion.15.clone.7.clone.5), kind=kOutput, calls=%fused_computation.49 | convolution fusion | flops 40645947392 | bytes 64070144 | tf_op jit(solution)/shard_map/bsf,fd->bsd/dot_general | solution.py:31
  1129.6 2.7 fusion.50
  1132.3 0.9 copy-done
  1133.2 44.9 %add_convert_fusion = bf16[32,128,3,16,72]{1,4,3,2,0:T(8,128)(2,1)} fusion(f32[3,16,72]{2,1,0:T(8,128)S(1)} %copy-done.4, bf16[32,128,1152]{2,1,0:T(8,128)(2,1)S(1)} %get-tuple-element.26, f32[1152]{0:T(1024)S(1)} %copy-done.15, f32[1152]{0:T(1024)S(1)} %copy-done.16, f32[32,128]{1,0:T(8,128)S(1)} %add_rsqrt_fusion.1, ...), kind=kOutput, calls=%fused_computation.28 | convolution fusion | flops 32671531008 | bytes 45767168 | tf_op jit(solution)/shard_map/bsd,dthe->bsthe/dot_general | solution.py:42
  1178.1 19.5 copy.25
  1197.6 316.2 %all_to_all.73 = bf16[32,128,3,16,72]{1,4,2,0,3:T(8,128)(2,1)} all-to-all(bf16[32,128,3,16,72]{1,4,2,0,3:T(8,128)(2,1)} %copy.25), channel_id=1, replica_groups=mesh['dp'=1,'sp'=8] {'sp'}, dimensions={3} | all-to-all | bytes 56623104 | tf_op jit(solution)/shard_map/all_to_all | solution.py:43
  1513.8 19.7 copy.38
  1533.5 41.8 %all_to_all.63 = bf16[32,1024,3,2,72]{1,4,3,0,2:T(8,128)(2,1)} reshape(bf16[32,8,128,3,2,72]{2,1,5,4,0,3:T(8,128)(2,1)} %bitcast.157) | data formatting | bytes 56623104 | tf_op jit(solution)/shard_map/all_to_all | solution.py:43
  1575.3 92.9 %multiply_reduce_fusion = (f32[32,2,1024]{2,1,0:T(2,128)S(1)}, f32[32,2,1024,1024]{2,3,1,0:T(8,128)}) fusion(bf16[32,1024,3,2,72]{1,4,3,0,2:T(8,128)(2,1)} %all_to_all.63), kind=kOutput, calls=%fused_computation.2 | convolution fusion | flops 9797828608 | bytes 287571968 | tf_op jit(solution)/shard_map/bqhe,bkhe->bhqk/dot_general | solution.py:19
  1668.2 80.7 %fusion.2 = f32[32,2,1024]{2,1,0:T(2,128)S(1)} fusion(f32[32,2,1024,1024]{2,3,1,0:T(8,128)} %get-tuple-element.28, f32[32,2,1024]{2,1,0:T(2,128)S(1)} %get-tuple-element.27), kind=kLoop, calls=%fused_computation.6 | loop fusion | flops 201261056 | bytes 268959744 | tf_op jit(solution)/shard_map/reduce_sum | solution.py:22
  1748.9 87.4 %divide_convert_fusion = bf16[32,2,1024,72]{2,3,1,0:T(8,128)(2,1)} fusion(f32[32,2,1024,1024]{2,3,1,0:T(8,128)} %get-tuple-element.28, f32[32,2,1024]{2,1,0:T(2,128)S(1)} %get-tuple-element.27, bf16[32,1024,3,2,72]{1,4,3,0,2:T(8,128)(2,1)} %all_to_all.63, f32[32,2,1024]{2,1,0:T(2,128)S(1)} %fusion.2), kind=kOutput, calls=%fused_computation.86 | convolution fusion | flops 9874440192 | bytes 287834112 | tf_op jit(solution)/shard_map/bhqk,bkhe->bhqe/dot_general | solution.py:23
  1836.3 36.8 %copy.28 = bf16[32,2,1024,72]{3,1,0,2:T(2,128)(2,1)} copy(bf16[32,2,1024,72]{2,3,1,0:T(8,128)(2,1)} %divide_convert_fusion) | data formatting | bytes 18874368 | tf_op jit(solution)/shard_map/convert_element_type | solution.py:24
  1873.1 190.0 %all_to_all.74 = bf16[32,2,1024,72]{3,1,0,2:T(2,128)(2,1)} all-to-all(bf16[32,2,1024,72]{3,1,0,2:T(2,128)(2,1)} %copy.28), channel_id=1, replica_groups=mesh['dp'=1,'sp'=8] {'sp'}, dimensions={2} | all-to-all | bytes 18874368 | tf_op jit(solution)/shard_map/all_to_all | solution.py:45
  2063.1 36.6 %copy.29 = bf16[32,2,8,128,72]{3,4,1,2,0:T(8,128)(2,1)} copy(bf16[32,2,8,128,72]{4,1,0,3,2:T(2,128)(2,1)} %bitcast.158) | data formatting | bytes 18874368 | tf_op jit(solution)/shard_map/all_to_all | solution.py:45
  2099.7 19.9 convert_reduce_fusion
  2119.7 2.8 fusion.46
  2122.5 72.5 %fusion.23.clone.11 = bf16[32,128,4304]{1,2,0:T(8,128)(2,1)} fusion(f32[4304]{0:T(1024)S(1)} %copy-done.5, bf16[32,128,1152]{2,1,0:T(8,128)(2,1)S(1)} %get-tuple-element.30, bf16[2,1152,4304]{1,2,0:T(8,128)(2,1)} %param.22, f32[1152]{0:T(1024)S(1)} %copy-done.14, f32[1152]{0:T(1024)S(1)} %copy-done.13, ...), kind=kOutput, calls=%fused_computation.27.clone.clone.clone.clone.clone.clone.clone.clone.clone.2 | convolution fusion | flops 40822243328 | bytes 54671168 | tf_op jit(solution)/shard_map/bsd,df->bsf/dot_general | solution.py:29
  2195.0 54.9 %fusion.71 = bf16[32,128,1152]{2,1,0:T(8,128)(2,1)} fusion(bf16[32,128,1152]{2,1,0:T(8,128)(2,1)S(1)} %get-tuple-element.30, bf16[2,4304,1152]{2,1,0:T(8,128)(2,1)} %param.24, f32[1152]{0:T(1024)S(1)} %copy-done.12, bf16[32,128,4304]{1,2,0:T(8,128)(2,1)} %fusion.23.clone.11), kind=kOutput, calls=%fused_computation.89 | convolution fusion | flops 40636514304 | bytes 64053760 | tf_op jit(solution)/shard_map/bsf,fd->bsd/dot_general | solution.py:31
  (43 shorter events, 0.1 us)
Async XLA Ops:
  0.0 12.9 slice-start
  0.0 12.9 slice-start.1
  0.0 11.6 copy-start.2
  0.0 12.3 copy-start.6
  0.0 12.3 copy-start.7
  5.2 7.8 slice-start.2
  753.8 4.8 copy-start.8
  753.8 5.5 copy-start.9
  753.8 6.1 copy-start.10
  753.8 6.1 copy-start.11
  753.8 6.7 copy-start.3
  753.9 188.8 %all-to-all-start.1 = ((bf16[32,2,1024,72]{3,1,0,2:T(2,128)(2,1)}), bf16[32,2,1024,72]{3,1,0,2:T(2,128)(2,1)}, u32[]{:S(2)}, u32[]{:S(2)}) async-start(bf16[32,2,1024,72]{3,1,0,2:T(2,128)(2,1)} %copy.23), calls=%async_computation.1 | async-start | bytes 33554432 | tf_op jit(solution)/shard_map/all_to_all | solution.py:45
  999.1 75.3 %copy-start.1 = (bf16[32,128,1152]{2,1,0:T(8,128)(2,1)}, bf16[32,128,1152]{2,1,0:T(8,128)(2,1)S(1)}, u32[]{:S(2)}) copy-start(bf16[32,128,1152]{2,1,0:T(8,128)(2,1)S(1)} %get-tuple-element.24) | copy-start | bytes 28311556
  1074.5 58.8 %copy-start.4 = (f32[3,16,72]{2,1,0:T(8,128)S(1)}, f32[3,16,72]{2,1,0:T(8,128)}, u32[]{:S(2)}) copy-start(f32[3,16,72]{2,1,0:T(8,128)} %get-tuple-element.19) | copy-start | bytes 41476
  1074.5 58.8 %copy-start.15 = (f32[1152]{0:T(1024)S(1)}, f32[1152]{0:T(1024)}, u32[]{:S(2)}) copy-start(f32[1152]{0:T(1024)} %get-tuple-element.17) | copy-start | bytes 13828
  1074.5 58.8 %copy-start.16 = (f32[1152]{0:T(1024)S(1)}, f32[1152]{0:T(1024)}, u32[]{:S(2)}) copy-start(f32[1152]{0:T(1024)} %get-tuple-element.32) | copy-start | bytes 13828
  1129.6 3.7 copy-start
  2063.1 36.6 %copy-start.17 = (f32[1152]{0:T(1024)S(1)}, f32[1152]{0:T(1024)}, u32[]{:S(2)}) copy-start(f32[1152]{0:T(1024)} %get-tuple-element.13) | copy-start | bytes 13828
  2099.7 22.7 %copy-start.5 = (f32[4304]{0:T(1024)S(1)}, f32[4304]{0:T(1024)}, u32[]{:S(2)}) copy-start(f32[4304]{0:T(1024)} %get-tuple-element.6) | copy-start | bytes 51652
  2099.7 22.7 %copy-start.13 = (f32[1152]{0:T(1024)S(1)}, f32[1152]{0:T(1024)}, u32[]{:S(2)}) copy-start(f32[1152]{0:T(1024)} %get-tuple-element.7) | copy-start | bytes 13828
  2099.7 22.7 %copy-start.14 = (f32[1152]{0:T(1024)S(1)}, f32[1152]{0:T(1024)}, u32[]{:S(2)}) copy-start(f32[1152]{0:T(1024)} %get-tuple-element.34) | copy-start | bytes 13828
  2122.5 72.5 %copy-start.12 = (f32[1152]{0:T(1024)S(1)}, f32[1152]{0:T(1024)}, u32[]{:S(2)}) copy-start(f32[1152]{0:T(1024)} %get-tuple-element.11) | copy-start | bytes 13828
where the time goes:
time: 2260 us; the launch traced here: 2250 us
  blocking collectives  824 us (36%)
  matrix products  745 us (33%)
  local copies, waits for them, and re-layouts  314 us (14%)
  other arithmetic  181 us (8%)
  waiting for transfers between devices  181 us (8%)
    all_to_all x2, blocking collectives, device_step(): qkv_heads = lax.all_to_all(qkv_local, 'sp', 3, 1, tiled=True)  634 us
    all_to_all x1, blocking collectives, device_step(): attn_tokens = lax.all_to_all(attn_heads, 'sp', 2, 1, tiled=True)  190 us
    dot_general x2, matrix products, attend(): jnp.einsum('bqhe,bkhe->bhqk', q_part, k_part, preferred_element_type=jnp....  186 us
    all_to_all x1, waiting for transfers between devices, device_step(): attn_tokens = lax.all_to_all(attn_heads, 'sp', 2, 1, tiled=True)  181 us
    dot_general x2, matrix products, attend(): jnp.einsum('bhqk,bkhe->bhqe', prob_vals.astype(jnp.bfloat16), v_part, pre...  175 us
    reduce_sum x2, other arithmetic, attend(): row_total = jnp.sum(prob_vals, axis=-1, keepdims=True)  161 us
    dot_general x2, matrix products, mlp_block(): jnp.einsum('bsd,df->bsf', normed, w_up, preferred_element_type=jnp.float32)  145 us
    all_to_all x4, local copies, waits for them, and re-layouts, device_step(): qkv_heads = lax.all_to_all(qkv_local, 'sp', 3, 1, tiled=True)  123 us
  transfers between devices with their start and end apart: 1, of which 1 were waited for; matrix products, arithmetic and copies ran while one was open for 0% of the time, Pallas kernels for 0%

commit v1 on v0

v1 whole, which is shorter than its diff:
```python
import functools
import math

import jax
import jax.numpy as jnp
from jax import lax
from jax.experimental import pallas as pl
from jax.experimental.pallas import tpu as pltpu
from jax.sharding import PartitionSpec as P

LN_EPS = 1e-6
LOG2E = math.log2(math.e)
VMEM_LIMIT = 60 * 1024 * 1024
BF16, F32 = jnp.bfloat16, jnp.float32


def layer_norm(tokens, gain, shift):
    values = tokens.astype(F32)
    mean_val = jnp.mean(values, axis=-1, keepdims=True)
    centred = values - mean_val
    var_val = jnp.mean(centred * centred, axis=-1, keepdims=True)
    return (centred * lax.rsqrt(var_val + LN_EPS) * gain + shift).astype(BF16)


def gelu_tanh(x):
    inner = x * (math.sqrt(2.0 / math.pi) + (math.sqrt(2.0 / math.pi) * 0.044715) * (x * x))
    half = 0.5 * x
    return half + half * jnp.tanh(inner)


def chunks(total, step):
    return [(start, min(step, total - start)) for start in range(0, total, step)]


def qkv_kernel(x_ref, gain_ref, shift_ref, w_ref, b_ref, o_ref, n_ref):
    parts, tile = x_ref.shape[0], x_ref.shape[2]
    per = n_ref.shape[1] // tile
    for sub in range(parts // per):
        for part in range(per):
            n_ref[sub, pl.ds(part * tile, tile), :] = layer_norm(x_ref[sub * per + part, 0], gain_ref[0], shift_ref[0])
    rows = n_ref.shape[1]
    for sub in range(parts // per):
        for start, size in chunks(w_ref.shape[2], 512):
            acc = jnp.dot(n_ref[sub], w_ref[0, :, pl.ds(start, size)], preferred_element_type=F32)
            o_ref[0, pl.ds(sub * rows, rows), pl.ds(start, size)] = (acc + b_ref[0, :, pl.ds(start, size)]).astype(BF16)


def attn_kernel(heads, head_dim, qkv_ref, x_ref, w_ref, b_ref, o_ref, vt_ref, ot_ref, of_ref, s_ref, p_ref):
    seq, width = qkv_ref.shape[1], heads * head_dim
    qb = s_ref.shape[2]
    scale = head_dim**-0.5 * LOG2E
    for start, size in chunks(width, 128):
        vt_ref[pl.ds(start, size), :] = qkv_ref[0, :, pl.ds(2 * width + start, size)].T

    lanes = lax.broadcasted_iota(jnp.int32, (1, 256), 1)
    pair_rows = 2 * head_dim

    def pair_body(pair, carry):
        units = [(hh, blk) for hh in range(2) for blk in range(seq // qb)]

        def scores(hh, blk, buf):
            first = (pair * 2 + hh) * head_dim
            off = pl.multiple_of(jnp.minimum(first // 128, width // 128 - 2) * 128, 128)
            mask = jnp.logical_and(lanes + off >= first, lanes + off < first + head_dim)
            k_win = qkv_ref[0, :, pl.ds(width + off, 256)]
            q_win = qkv_ref[0, pl.ds(blk * qb, qb), pl.ds(off, 256)]
            q_win = jnp.where(mask, q_win, jnp.zeros_like(q_win))
            s_ref[buf] = lax.dot_general(k_win, q_win, (((1,), (1,)), ((), ())), preferred_element_type=F32)

        def finish(hh, blk, buf):
            step = 64
            peak = s_ref[buf, pl.ds(0, 8), :]
            for r in range(8, seq, 8):
                peak = jnp.maximum(peak, s_ref[buf, pl.ds(r, 8), :])
            peak = jnp.max(peak, axis=0, keepdims=True)
            total = jnp.zeros((8, qb), F32)
            for r in range(0, seq, step):
                prob = jnp.exp2((s_ref[buf, pl.ds(r, step), :] - peak) * scale)
                p_ref[buf, pl.ds(r, step), :] = prob.astype(BF16)
                for g in range(0, step, 8):
                    total = total + prob[g : g + 8]
            total = jnp.sum(total, axis=0, keepdims=True)
            v_rows = pl.multiple_of(pair * pair_rows + 64 * hh, 16)
            mixed = jnp.dot(vt_ref[pl.ds(v_rows, 80), :], p_ref[buf], preferred_element_type=F32)
            mixed = mixed[8 * hh : 8 * hh + head_dim] * (1.0 / total)
            of_ref[pl.ds(hh * head_dim, head_dim), pl.ds(blk * qb, qb)] = mixed

        scores(*units[0], 0)
        for i, unit in enumerate(units):
            if i + 1 < len(units):
                scores(*units[i + 1], (i + 1) % 2)
            finish(*unit, i % 2)
        ot_ref[pl.ds(pl.multiple_of(pair * pair_rows, 16), pair_rows), :] = of_ref[...].astype(BF16)
        return carry

    lax.fori_loop(0, heads // 2, pair_body, 0)

    tile = x_ref.shape[2]
    for part in range(x_ref.shape[0]):
        o_part = ot_ref[:, pl.ds(part * tile, tile)].T
        acc = jnp.dot(o_part, w_ref[0], preferred_element_type=F32) + b_ref[0]
        o_ref[part, 0] = (x_ref[part, 0].astype(F32) + acc).astype(BF16)


def mlp_kernel(x_ref, gain_ref, shift_ref, wu_ref, bu_ref, wd_ref, bd_ref, o_ref, n_ref, a_ref):
    parts, tile = x_ref.shape[0], x_ref.shape[2]
    per = n_ref.shape[1] // tile
    for sub in range(parts // per):
        for part in range(per):
            n_ref[sub, pl.ds(part * tile, tile), :] = layer_norm(x_ref[sub * per + part, 0], gain_ref[0], shift_ref[0])
    for sub in range(parts // per):
        for start, size in chunks(wu_ref.shape[2], 512):
            acc = jnp.dot(n_ref[sub], wu_ref[0, :, pl.ds(start, size)], preferred_element_type=F32)
            a_ref[sub, :, pl.ds(start, size)] = gelu_tanh(acc + bu_ref[0, :, pl.ds(start, size)]).astype(BF16)
        acc = jnp.dot(a_ref[sub], wd_ref[0], preferred_element_type=F32) + bd_ref[0]
        for part in range(per):
            mid = x_ref[sub * per + part, 0].astype(F32)
            o_ref[sub * per + part, 0] = (mid + acc[part * tile : (part + 1) * tile]).astype(BF16)


def resident(shape, layer):
    return pl.BlockSpec((1,) + shape[1:], lambda *ids: (layer,) + (0,) * (len(shape) - 1), pipeline_mode=pl.Buffered(1))


def solution(mesh):
    token_spec = P('dp', 'sp', None)
    n = mesh.shape['sp']

    def device_step(image_tokens, ln1_gain, ln1_shift, w_qkv, b_qkv, w_out, b_out, ln2_gain, ln2_shift, w_up, b_up, w_down, b_down):
        images, tile, width = image_tokens.shape
        layers, _, _, heads, head_dim = w_qkv.shape
        mlp = w_up.shape[2]
        own, seq = images // n, n * tile
        row = lambda a: a.reshape(layers, 1, -1)
        w_qkv = w_qkv.reshape(layers, width, 3 * width)
        w_out = w_out.reshape(layers, width, width)
        ln1_gain, ln1_shift, b_qkv, b_out, ln2_gain, ln2_shift, b_up, b_down = map(
            row, (ln1_gain, ln1_shift, b_qkv, b_out, ln2_gain, ln2_shift, b_up, b_down)
        )
        tokens = image_tokens.shape[0] * tile
        params = pltpu.CompilerParams(vmem_limit_bytes=VMEM_LIMIT)
        half = n // 2
        h_shape = jax.ShapeDtypeStruct((n, own, tile, width), BF16)

        def qkv(h, layer):
            return pl.pallas_call(
                qkv_kernel,
                grid=(own, 2),
                out_shape=jax.ShapeDtypeStruct((own, seq, 3 * width), BF16),
                in_specs=[pl.BlockSpec((half, 1, tile, width), lambda i, j: (j, i, 0, 0))]
                + [resident(a.shape, layer) for a in (ln1_gain, ln1_shift, w_qkv, b_qkv)],
                out_specs=pl.BlockSpec((1, seq // 2, 3 * width), lambda i, j: (i, j, 0)),
                scratch_shapes=[pltpu.VMEM((2, seq // 4, width), BF16)],
                compiler_params=params,
                cost_estimate=pl.CostEstimate(flops=2 * tokens * width * 3 * width, bytes_accessed=2 * tokens * width * 4, transcendentals=0),
                name='qkv',
            )(h, ln1_gain, ln1_shift, w_qkv, b_qkv)

        def attend(qkv_all, h, layer):
            return pl.pallas_call(
                functools.partial(attn_kernel, heads, head_dim),
                grid=(own,),
                out_shape=h_shape,
                in_specs=[
                    pl.BlockSpec((1, seq, 3 * width), lambda i: (i, 0, 0)),
                    pl.BlockSpec((n, 1, tile, width), lambda i: (0, i, 0, 0)),
                    resident(w_out.shape, layer),
                    resident(b_out.shape, layer),
                ],
                out_specs=pl.BlockSpec((n, 1, tile, width), lambda i: (0, i, 0, 0)),
                scratch_shapes=[
                    pltpu.VMEM((width, seq), BF16),
                    pltpu.VMEM((width, seq), BF16),
                    pltpu.VMEM((2 * head_dim, seq), F32),
                    pltpu.VMEM((2, seq, 256), F32),
                    pltpu.VMEM((2, seq, 256), BF16),
                ],
                compiler_params=params,
                cost_estimate=pl.CostEstimate(
                    flops=4 * tokens * width * seq + 2 * tokens * width * width,
                    bytes_accessed=2 * tokens * width * 5,
                    transcendentals=tokens * heads * seq,
                ),
                name='attend',
            )(qkv_all, h, w_out, b_out)

        def mlp_layer(h, layer):
            return pl.pallas_call(
                mlp_kernel,
                grid=(own, 2),
                out_shape=h_shape,
                in_specs=[pl.BlockSpec((half, 1, tile, width), lambda i, j: (j, i, 0, 0))]
                + [resident(a.shape, layer) for a in (ln2_gain, ln2_shift, w_up, b_up, w_down, b_down)],
                out_specs=pl.BlockSpec((half, 1, tile, width), lambda i, j: (j, i, 0, 0)),
                scratch_shapes=[pltpu.VMEM((2, seq // 4, width), BF16), pltpu.VMEM((2, seq // 4, mlp), BF16)],
                compiler_params=params,
                cost_estimate=pl.CostEstimate(flops=4 * tokens * width * mlp, bytes_accessed=2 * tokens * width * 2, transcendentals=tokens * mlp),
                name='mlp',
            )(h, ln2_gain, ln2_shift, w_up, b_up, w_down, b_down)

        h = lax.all_to_all(image_tokens.reshape(n, own, tile, width), 'sp', 0, 0)
        for layer in range(layers):
            h = mlp_layer(attend(qkv(h, layer), h, layer), layer)
        h = lax.all_to_all(h, 'sp', 0, 0)
        return h.reshape(images, tile, width)

    return jax.shard_map(device_step, mesh=mesh, in_specs=(token_spec,) + (P(),) * 12, out_specs=token_spec, check_vma=False)
```

time: 2260 us -> 806 us (0.36)
  matrix products: 745 us -> 0 us
  blocking collectives: 824 us -> 110 us
  Pallas kernels: 0 us -> 572 us
  local copies, waits for them, and re-layouts: 314 us -> 59.7 us
  other arithmetic: 181 us -> 0 us
  waiting for transfers between devices: 181 us -> 54.6 us
    dot_general x12 -> x0, matrix products: 745 us -> none  [the longest x2 186 us: attend(): jnp.einsum('bqhe,bkhe->bhqk', q_part, k_part, preferred_element_type=jnp....]
    all_to_all x3 -> x1, blocking collectives: 824 us -> 110 us  [device_step(): h = lax.all_to_all(h, 'sp', 0, 0)]
    pallas_call x0 -> x6, Pallas kernels: none -> 572 us  [the longest x2 255 us: attend(): pl.pallas_call(functools.partial(attn_kernel, heads, head_dim), grid=(own...]
    all_to_all x6 -> x0, local copies, waits for them, and re-layouts: 196 us -> none  [the longest x4 123 us: device_step(): qkv_heads = lax.all_to_all(qkv_local, 'sp', 3, 1, tiled=True)]
    reduce_sum x7 -> x0, other arithmetic: 181 us -> none  [the longest x2 161 us: attend(): row_total = jnp.sum(prob_vals, axis=-1, keepdims=True)]
    all_to_all x1, waiting for transfers between devices: 181 us -> 54.6 us  [device_step(): h = lax.all_to_all(image_tokens.reshape(n, own, tile, width), 'sp', 0, 0)]
    convert_element_type x4 -> x0, local copies, waits for them, and re-layouts: 113 us -> none  [the longest x2 73.7 us: attend(): return (mixed_vals / row_total).astype(jnp.bfloat16)]
    unnamed x42 -> x18, local copies, waits for them, and re-layouts: 0.99 us -> 34.1 us
  transfers between devices with their start and end apart: 1 -> 1, of which waited for: 1 -> 1; matrix products, arithmetic and copies ran while one was open for 0% -> 6% of each run, Pallas kernels for 0% -> 0%
where the time goes in v1:
time: 806 us; the launch traced here: 801 us
  Pallas kernels  572 us (71%)
  blocking collectives  110 us (14%)
  local copies, waits for them, and re-layouts  59.7 us (7%)
  waiting for transfers between devices  54.6 us (7%)
    pallas_call x2, Pallas kernels, attend(): pl.pallas_call(functools.partial(attn_kernel, heads, head_dim), grid=(own...  255 us
    pallas_call x2, Pallas kernels, mlp_layer(): pl.pallas_call(mlp_kernel, grid=(own, 2), out_shape=h_shape, in_specs=[pl...  221 us
    all_to_all x1, blocking collectives, device_step(): h = lax.all_to_all(h, 'sp', 0, 0)  110 us
    pallas_call x2, Pallas kernels, qkv(): pl.pallas_call(qkv_kernel, grid=(own, 2), out_shape=jax.ShapeDtypeStruct(...  95.7 us
    all_to_all x1, waiting for transfers between devices, device_step(): h = lax.all_to_all(image_tokens.reshape(n, own, tile, width), 'sp', 0, 0)  54.6 us
    unnamed x18, local copies, waits for them, and re-layouts  34.1 us
    reshape x1, local copies, waits for them, and re-layouts, device_step(): w_qkv = w_qkv.reshape(layers, width, 3 * width)  20.6 us
  transfers between devices with their start and end apart: 1, of which 1 were waited for; matrix products, arithmetic and copies ran while one was open for 6% of the time, Pallas kernels for 0%

profile of v1, /device:TPU:0, one launch (start us, length us, event | category | flops | bytes accessed | tf_op | source)
XLA Modules:
  0.0 800.5 jit_solution(10770991100894373072)
XLA Ops:
  0.0 4.3 all-to-all-start
  4.3 0.0 copy-start
  4.3 0.0 copy-start.2
  4.3 0.0 copy-start.3
  4.3 0.0 copy-start.4
  4.3 20.6 %copy.17.w_ref = bf16[2,1152,3456]{2,1,0:T(8,128)(2,1)} copy(bf16[2,1152,3456]{1,2,0:T(8,128)(2,1)} %bitcast.7) | data formatting | bytes 31850496 | tf_op jit(solution)/shard_map/reshape | solution.py:135
  24.9 0.0 copy-done
  24.9 0.7 reshape.40.b_ref
  25.7 0.0 copy-done.2
  25.7 0.6 reshape.37.gain_ref
  26.3 0.0 copy-done.3
  26.3 0.6 reshape.38.shift_ref
  26.9 0.0 copy-done.4
  26.9 0.6 reshape.42.b_ref
  27.5 0.0 copy-start.1
  27.5 0.0 copy-start.5
  27.5 0.0 copy-start.6
  27.5 0.0 copy-start.7
  27.5 25.5 %copy.18.wu_ref = bf16[2,1152,4304]{2,1,0:T(8,128)(2,1)} copy(bf16[2,1152,4304]{1,2,0:T(8,128)(2,1)} %param.22) | data formatting | bytes 39665664 | tf_op args[9]
  53.0 0.0 copy-done.1
  53.0 0.6 reshape.45.bu_ref
  53.6 0.0 copy-done.5
  53.6 0.6 reshape.43.gain_ref
  54.2 0.0 copy-done.6
  54.2 0.6 reshape.44.shift_ref
  54.8 0.0 copy-done.7
  54.8 0.6 reshape.46.bd_ref
  55.4 54.6 %all-to-all-done.x_ref = bf16[8,4,128,1152]{3,2,1,0:T(8,128)(2,1)} async-done(((bf16[8,4,128,1152]{3,2,1,0:T(8,128)(2,1)}), bf16[8,4,128,1152]{3,2,1,0:T(8,128)(2,1)}, u32[]{:S(2)}, u32[]{:S(2)}) %all-to-all-start) | async-done | bytes 9437216 | tf_op jit(solution)/shard_map/all_to_all | solution.py:201
  110.1 47.8 %qkv.2.qkv_ref = bf16[4,1024,3456]{2,1,0:T(8,128)(2,1)} custom-call(bf16[8,4,128,1152]{3,2,1,0:T(8,128)(2,1)} %all-to-all-done.x_ref, f32[2,1,1152]{2,1,0:T(1,128)} %reshape.37.gain_ref, f32[2,1,1152]{2,1,0:T(1,128)} %reshape.38.shift_ref, bf16[2,1152,3456]{2,1,0:T(8,128)(2,1)} %copy.17.w_ref, f32[2,1,3456]{2,1,0:T(1,128)} %reshape.40.b_ref), custom_call_target="tpu_custom_call" | custom-call | flops 32614907904 | bytes 37748736 | tf_op jit(solution)/shard_map/qkv/pallas_call | solution.py:146
  157.9 128.0 %attend.2.x_ref = bf16[8,4,128,1152]{3,2,1,0:T(8,128)(2,1)} custom-call(bf16[4,1024,3456]{2,1,0:T(8,128)(2,1)} %qkv.2.qkv_ref, bf16[8,4,128,1152]{3,2,1,0:T(8,128)(2,1)} %all-to-all-done.x_ref, bf16[2,1152,1152]{2,1,0:T(8,128)(2,1)} %bitcast.9, f32[2,1,1152]{2,1,0:T(1,128)} %reshape.42.b_ref), custom_call_target="tpu_custom_call" | custom-call | flops 30198988800 | bytes 47185920 | tf_op jit(solution)/shard_map/attend/pallas_call | solution.py:160
  285.9 110.2 %mlp.2.x_ref = bf16[8,4,128,1152]{3,2,1,0:T(8,128)(2,1)} custom-call(bf16[8,4,128,1152]{3,2,1,0:T(8,128)(2,1)} %attend.2.x_ref, f32[2,1,1152]{2,1,0:T(1,128)} %reshape.43.gain_ref, f32[2,1,1152]{2,1,0:T(1,128)} %reshape.44.shift_ref, bf16[2,1152,4304]{2,1,0:T(8,128)(2,1)} %copy.18.wu_ref, f32[2,1,4304]{2,1,0:T(1,128)} %reshape.45.bu_ref, ...), custom_call_target="tpu_custom_call" | custom-call | flops 81235279872 | bytes 18874368 | tf_op jit(solution)/shard_map/mlp/pallas_call | solution.py:188
  396.0 48.0 %qkv.3.qkv_ref = bf16[4,1024,3456]{2,1,0:T(8,128)(2,1)} custom-call(bf16[8,4,128,1152]{3,2,1,0:T(8,128)(2,1)} %mlp.2.x_ref, f32[2,1,1152]{2,1,0:T(1,128)} %reshape.37.gain_ref, f32[2,1,1152]{2,1,0:T(1,128)} %reshape.38.shift_ref, bf16[2,1152,3456]{2,1,0:T(8,128)(2,1)} %copy.17.w_ref, f32[2,1,3456]{2,1,0:T(1,128)} %reshape.40.b_ref), custom_call_target="tpu_custom_call" | custom-call | flops 32614907904 | bytes 37748736 | tf_op jit(solution)/shard_map/qkv/pallas_call | solution.py:146
  444.0 127.5 %attend.3.x_ref = bf16[8,4,128,1152]{3,2,1,0:T(8,128)(2,1)} custom-call(bf16[4,1024,3456]{2,1,0:T(8,128)(2,1)} %qkv.3.qkv_ref, bf16[8,4,128,1152]{3,2,1,0:T(8,128)(2,1)} %mlp.2.x_ref, bf16[2,1152,1152]{2,1,0:T(8,128)(2,1)} %bitcast.10, f32[2,1,1152]{2,1,0:T(1,128)} %reshape.42.b_ref), custom_call_target="tpu_custom_call" | custom-call | flops 30198988800 | bytes 47185920 | tf_op jit(solution)/shard_map/attend/pallas_call | solution.py:160
  571.5 110.4 %mlp.3 = bf16[8,4,128,1152]{3,2,1,0:T(8,128)(2,1)} custom-call(bf16[8,4,128,1152]{3,2,1,0:T(8,128)(2,1)} %attend.3.x_ref, f32[2,1,1152]{2,1,0:T(1,128)} %reshape.43.gain_ref, f32[2,1,1152]{2,1,0:T(1,128)} %reshape.44.shift_ref, bf16[2,1152,4304]{2,1,0:T(8,128)(2,1)} %copy.18.wu_ref, f32[2,1,4304]{2,1,0:T(1,128)} %reshape.45.bu_ref, ...), custom_call_target="tpu_custom_call" | custom-call | flops 81235279872 | bytes 18874368 | tf_op jit(solution)/shard_map/mlp/pallas_call | solution.py:188
  681.8 109.7 %all_to_all.10 = bf16[8,4,128,1152]{3,2,1,0:T(8,128)(2,1)} all-to-all(bf16[8,4,128,1152]{3,2,1,0:T(8,128)(2,1)} %mlp.3), channel_id=1, replica_groups=mesh['dp'=1,'sp'=8] {'sp'}, dimensions={0} | all-to-all | bytes 18874368 | tf_op jit(solution)/shard_map/all_to_all | solution.py:204
  791.5 8.6 %copy.22 = bf16[32,128,1152]{2,1,0:T(8,128)(2,1)} copy(bf16[32,128,1152]{2,1,0:T(8,128)(2,1)} %bitcast.6) | data formatting | bytes 18874368
Async XLA Ops:
  0.0 110.1 %all-to-all-start = ((bf16[8,4,128,1152]{3,2,1,0:T(8,128)(2,1)}), bf16[8,4,128,1152]{3,2,1,0:T(8,128)(2,1)}, u32[]{:S(2)}, u32[]{:S(2)}) async-start(bf16[8,4,128,1152]{3,2,1,0:T(8,128)(2,1)} %bitcast.8), calls=%async_computation | async-start | bytes 18874368 | tf_op jit(solution)/shard_map/all_to_all | solution.py:201
  4.3 20.6 %copy-start = (f32[2,3,16,72]{3,2,1,0:T(8,128)S(1)}, f32[2,3,16,72]{3,2,1,0:T(8,128)}, u32[]{:S(2)}) copy-start(f32[2,3,16,72]{3,2,1,0:T(8,128)} %param.17) | copy-start | bytes 82948
  4.3 21.4 %copy-start.2 = (f32[2,1152]{1,0:T(2,128)S(1)}, f32[2,1152]{1,0:T(2,128)}, u32[]{:S(2)}) copy-start(f32[2,1152]{1,0:T(2,128)} %param.14) | copy-start | bytes 27652
  4.3 22.0 %copy-start.3 = (f32[2,1152]{1,0:T(2,128)S(1)}, f32[2,1152]{1,0:T(2,128)}, u32[]{:S(2)}) copy-start(f32[2,1152]{1,0:T(2,128)} %param.15) | copy-start | bytes 27652
  4.3 22.6 %copy-start.4 = (f32[2,1152]{1,0:T(2,128)S(1)}, f32[2,1152]{1,0:T(2,128)}, u32[]{:S(2)}) copy-start(f32[2,1152]{1,0:T(2,128)} %param.19) | copy-start | bytes 27652
  27.5 25.5 %copy-start.1 = (f32[2,4304]{1,0:T(2,128)S(1)}, f32[2,4304]{1,0:T(2,128)}, u32[]{:S(2)}) copy-start(f32[2,4304]{1,0:T(2,128)} %param.23) | copy-start | bytes 103300
  27.5 26.1 %copy-start.5 = (f32[2,1152]{1,0:T(2,128)S(1)}, f32[2,1152]{1,0:T(2,128)}, u32[]{:S(2)}) copy-start(f32[2,1152]{1,0:T(2,128)} %param.20) | copy-start | bytes 27652
  27.5 26.7 %copy-start.6 = (f32[2,1152]{1,0:T(2,128)S(1)}, f32[2,1152]{1,0:T(2,128)}, u32[]{:S(2)}) copy-start(f32[2,1152]{1,0:T(2,128)} %param.21) | copy-start | bytes 27652
  27.5 27.3 %copy-start.7 = (f32[2,1152]{1,0:T(2,128)S(1)}, f32[2,1152]{1,0:T(2,128)}, u32[]{:S(2)}) copy-start(f32[2,1152]{1,0:T(2,128)} %param.25) | copy-start | bytes 27652

commit v2 on v0

v2 whole, which is shorter than its diff:
```python
import functools
import math

import jax
import jax.numpy as jnp
from jax import lax
from jax.experimental import pallas as pl
from jax.experimental.pallas import tpu as pltpu
from jax.sharding import PartitionSpec as P

LN_EPS = 1e-6
LOG2E = math.log2(math.e)
VMEM_LIMIT = 67_043_328
BF16, F32 = jnp.bfloat16, jnp.float32
MESH = pl.DeviceIdType.MESH
NT = (((1,), (1,)), ((), ()))


def layer_norm(tokens, gain, shift):
    values = tokens.astype(F32)
    mean_val = jnp.mean(values, axis=-1, keepdims=True)
    centred = values - mean_val
    var_val = jnp.mean(centred * centred, axis=-1, keepdims=True)
    return (centred * lax.rsqrt(var_val + LN_EPS) * gain + shift).astype(BF16)


def gelu_tanh(x):
    inner = x * (math.sqrt(2.0 / math.pi) + (math.sqrt(2.0 / math.pi) * 0.044715) * (x * x))
    half = 0.5 * x
    return half + half * jnp.tanh(inner)


def chunks(total, step):
    return [(start, min(step, total - start)) for start in range(0, total, step)]


def encoder_kernel(
    n, layers, heads, head_dim,
    x_hbm, g1_ref, s1_ref, wqkv_hbm, bqkv_ref, wout_hbm, bout_ref, g2_ref, s2_ref, wup_hbm, bup_ref, wdown_hbm, bdown_ref,
    out_hbm,
    h_ref, wqkv_ref, wout_ref, wup_ref, wdown_ref, qkv_ref, vt_ref, ot_ref, of_ref, s_ref, p_ref, n_ref, a_ref,
    w_sem, in_send, in_recv, out_send, out_recv,
):
    own, _, tile, width = h_ref.shape
    seq = n * tile
    mlp = wup_ref.shape[0]
    rows = n_ref.shape[0]
    per = rows // tile
    tiles = n // per
    qb = s_ref.shape[2]
    me = lax.axis_index('sp')
    dp = lax.axis_index('dp')

    def weight_copy(which, layer):
        src, dst = ((wqkv_hbm, wqkv_ref), (wout_hbm, wout_ref), (wup_hbm, wup_ref), (wdown_hbm, wdown_ref))[which]
        return pltpu.make_async_copy(src.at[layer], dst, w_sem.at[which])

    def send_in(image, peer):
        return pltpu.make_async_remote_copy(
            src_ref=x_hbm.at[peer * own + image], dst_ref=h_ref.at[image, me],
            send_sem=in_send.at[image, peer], recv_sem=in_recv.at[image, me], device_id=(dp, peer), device_id_type=MESH)

    def keep_in(image):
        return pltpu.make_async_copy(x_hbm.at[me * own + image], h_ref.at[image, me], in_recv.at[image, me])

    def send_out(image, peer):
        return pltpu.make_async_remote_copy(
            src_ref=h_ref.at[image, peer], dst_ref=out_hbm.at[me * own + image],
            send_sem=out_send.at[image, peer], recv_sem=out_recv.at[image, me], device_id=(dp, peer), device_id_type=MESH)

    def keep_out(image):
        return pltpu.make_async_copy(h_ref.at[image, me], out_hbm.at[me * own + image], out_recv.at[image, me])

    for which in range(4):
        weight_copy(which, 0).start()

    barrier = pltpu.get_barrier_semaphore()
    for k in range(1, n):
        pl.semaphore_signal(barrier, inc=1, device_id=(dp, lax.rem(me + k, n)), device_id_type=MESH)
    pl.semaphore_wait(barrier, n - 1)

    def start_in(image, carry):
        keep_in(image).start()

        def one(k, c):
            send_in(image, lax.rem(me + k, n)).start()
            return c

        return lax.fori_loop(1, n, one, carry)

    lax.fori_loop(0, own, start_in, 0)

    lanes = lax.broadcasted_iota(jnp.int32, (1, 256), 1)
    pair_rows = 2 * head_dim
    scale = head_dim**-0.5 * LOG2E
    last_window = width // 128 - 2
    pairs = heads // 2
    units = [(hh, blk) for hh in range(2) for blk in range(seq // qb)]

    def scores(pair, hh, blk, buf):
        first = (pair * 2 + hh) * head_dim
        off = pl.multiple_of(jnp.minimum(first // 128, last_window) * 128, 128)
        mask = jnp.logical_and(lanes + off >= first, lanes + off < first + head_dim)
        q_win = qkv_ref[pl.ds(blk * qb, qb), pl.ds(off, 256)]
        q_win = jnp.where(mask, q_win, jnp.zeros_like(q_win))
        for half in range(2):
            k_win = qkv_ref[pl.ds(half * (seq // 2), seq // 2), pl.ds(width + off, 256)]
            s_ref[buf, pl.ds(half * (seq // 2), seq // 2), :] = lax.dot_general(k_win, q_win, NT, preferred_element_type=F32)

    def finish(pair, hh, blk, buf):
        peak = jnp.max(s_ref[buf], axis=0, keepdims=True)
        total = jnp.zeros((1, qb), F32)
        for start, size in chunks(seq, 256):
            prob = jnp.exp2((s_ref[buf, pl.ds(start, size), :] - peak) * scale)
            p_ref[buf, pl.ds(start, size), :] = prob.astype(BF16)
            total = total + jnp.sum(prob, axis=0, keepdims=True)
        lane0 = jnp.minimum(pair * pair_rows // 128, last_window) * 128
        v_rows = pl.multiple_of(pair * pair_rows - lane0 + 64 * hh, 16)
        mixed = jnp.dot(vt_ref[pl.ds(v_rows, 80), :], p_ref[buf], preferred_element_type=F32)
        of_ref[pl.ds(hh * head_dim, head_dim), pl.ds(blk * qb, qb)] = mixed[8 * hh : 8 * hh + head_dim] * (1.0 / total)

    def pair_body(pair, carry):
        lane0 = pl.multiple_of(jnp.minimum(pair * pair_rows // 128, last_window) * 128, 128)
        vt_ref[...] = qkv_ref[:, pl.ds(2 * width + lane0, 256)].T
        following = jnp.minimum(pair + 1, pairs - 1)
        for i, (hh, blk) in enumerate(units):
            if i + 1 < len(units):
                scores(pair, *units[i + 1], (i + 1) % 2)
            else:
                scores(following, *units[0], (i + 1) % 2)
            finish(pair, hh, blk, i % 2)
        ot_ref[pl.ds(pl.multiple_of(pair * pair_rows, 16), pair_rows), :] = of_ref[...].astype(BF16)
        return carry

    def step(g, carry):
        layer, image = g // own, lax.rem(g, own)

        @pl.when(image == 0)
        def _():
            weight_copy(0, layer).wait()

        @pl.when(layer == 0)
        def _():
            keep_in(image).wait()
            for k in range(1, n):
                src = lax.rem(me + n - k, n)
                pltpu.make_async_remote_copy(
                    src_ref=x_hbm.at[image], dst_ref=h_ref.at[image, src], send_sem=in_send.at[image, src],
                    recv_sem=in_recv.at[image, src], device_id=(dp, src), device_id_type=MESH).wait_recv()

        def next_layer(which):
            @pl.when(jnp.logical_and(image == own - 1, layer < layers - 1))
            def _():
                weight_copy(which, layer + 1).start()

        def qkv_tile(t, c):
            tokens = h_ref[image, pl.ds(t * per, per)].reshape(rows, width)
            n_ref[...] = layer_norm(tokens, g1_ref[layer], s1_ref[layer])
            at = pl.ds(pl.multiple_of(t * rows, rows), rows)
            for start, size in chunks(3 * width, 512):
                acc = lax.dot_general(n_ref[...], wqkv_ref[pl.ds(start, size), :], NT, preferred_element_type=F32)
                qkv_ref[at, pl.ds(start, size)] = (acc + bqkv_ref[layer, :, pl.ds(start, size)]).astype(BF16)
            return c

        lax.fori_loop(0, tiles, qkv_tile, 0)
        next_layer(0)
        scores(0, *units[0], 0)
        lax.fori_loop(0, pairs, pair_body, 0)

        @pl.when(image == 0)
        def _():
            for which in range(1, 4):
                weight_copy(which, layer).wait()

        def mlp_tile(t, c):
            blocks = pl.ds(t * per, per)
            at = pl.ds(pl.multiple_of(t * rows, rows), rows)
            acc = jnp.dot(ot_ref[:, at].T, wout_ref[...], preferred_element_type=F32) + bout_ref[layer]
            mid = (h_ref[image, blocks].reshape(rows, width).astype(F32) + acc).astype(BF16)
            h_ref[image, blocks] = mid.reshape(per, tile, width)
            n_ref[...] = layer_norm(mid, g2_ref[layer], s2_ref[layer])
            for start, size in chunks(mlp, 512):
                acc = lax.dot_general(n_ref[...], wup_ref[pl.ds(start, size), :], NT, preferred_element_type=F32)
                a_ref[:, pl.ds(start, size)] = gelu_tanh(acc + bup_ref[layer, :, pl.ds(start, size)]).astype(BF16)
            acc = jnp.dot(a_ref[...], wdown_ref[...], preferred_element_type=F32) + bdown_ref[layer]
            new = h_ref[image, blocks].reshape(rows, width).astype(F32) + acc
            h_ref[image, blocks] = new.astype(BF16).reshape(per, tile, width)

            @pl.when(layer == layers - 1)
            def _():
                for part in range(per):
                    peer = t * per + part

                    @pl.when(peer == me)
                    def _():
                        keep_out(image).start()

                    @pl.when(peer != me)
                    def _():
                        send_out(image, peer).start()

            return c

        lax.fori_loop(0, tiles, mlp_tile, 0)
        for which in range(1, 4):
            next_layer(which)
        return carry

    lax.fori_loop(0, layers * own, step, 0)

    def drain(image, carry):
        keep_out(image).wait()
        for k in range(1, n):
            peer = lax.rem(me + k, n)
            send_in(image, peer).wait_send()
            send_out(image, peer).wait_send()
            pltpu.make_async_remote_copy(
                src_ref=h_ref.at[image, peer], dst_ref=out_hbm.at[peer * own + image], send_sem=out_send.at[image, peer],
                recv_sem=out_recv.at[image, peer], device_id=(dp, peer), device_id_type=MESH).wait_recv()
        return carry

    lax.fori_loop(0, own, drain, 0)


def solution(mesh):
    token_spec = P('dp', 'sp', None)
    n = mesh.shape['sp']

    def device_step(image_tokens, ln1_gain, ln1_shift, w_qkv, b_qkv, w_out, b_out, ln2_gain, ln2_shift, w_up, b_up, w_down, b_down):
        images, tile, width = image_tokens.shape
        layers, _, _, heads, head_dim = w_qkv.shape
        mlp = w_up.shape[2]
        own, seq = images // n, n * tile
        row = lambda a: a.reshape(layers, 1, -1)
        w_qkv = jnp.swapaxes(w_qkv.reshape(layers, width, 3 * width), 1, 2)
        w_up = jnp.swapaxes(w_up, 1, 2)
        w_out = w_out.reshape(layers, width, width)
        hbm = pl.BlockSpec(memory_space=pl.ANY)
        vmem = pl.BlockSpec(memory_space=pltpu.VMEM)
        rows = seq // 2
        return pl.pallas_call(
            functools.partial(encoder_kernel, n, layers, heads, head_dim),
            out_shape=jax.ShapeDtypeStruct(image_tokens.shape, BF16),
            in_specs=[hbm, vmem, vmem, hbm, vmem, hbm, vmem, vmem, vmem, hbm, vmem, hbm, vmem],
            out_specs=hbm,
            scratch_shapes=[
                pltpu.VMEM((own, n, tile, width), BF16),
                pltpu.VMEM((3 * width, width), BF16),
                pltpu.VMEM((width, width), BF16),
                pltpu.VMEM((mlp, width), BF16),
                pltpu.VMEM((mlp, width), BF16),
                pltpu.VMEM((seq, 3 * width), BF16),
                pltpu.VMEM((256, seq), BF16),
                pltpu.VMEM((width, seq), BF16),
                pltpu.VMEM((2 * head_dim, seq), F32),
                pltpu.VMEM((2, seq, 256), F32),
                pltpu.VMEM((2, seq, 256), BF16),
                pltpu.VMEM((rows, width), BF16),
                pltpu.VMEM((rows, mlp), BF16),
                pltpu.SemaphoreType.DMA((4,)),
                pltpu.SemaphoreType.DMA((own, n)),
                pltpu.SemaphoreType.DMA((own, n)),
                pltpu.SemaphoreType.DMA((own, n)),
                pltpu.SemaphoreType.DMA((own, n)),
            ],
            compiler_params=pltpu.CompilerParams(vmem_limit_bytes=VMEM_LIMIT, collective_id=0, has_side_effects=True),
            name='encoder',
        )(
            image_tokens, row(ln1_gain), row(ln1_shift), w_qkv, row(b_qkv), w_out, row(b_out),
            row(ln2_gain), row(ln2_shift), w_up, row(b_up), w_down, row(b_down),
        )

    return jax.shard_map(device_step, mesh=mesh, in_specs=(token_spec,) + (P(),) * 12, out_specs=token_spec, check_vma=False)
```

time: 2260 us -> 575 us (0.25)
  blocking collectives: 824 us -> 0 us
  matrix products: 745 us -> 0 us
  Pallas kernels: 0 us -> 555 us
  local copies, waits for them, and re-layouts: 314 us -> 19.3 us
  other arithmetic: 181 us -> 0 us
  waiting for transfers between devices: 181 us -> 0 us
    all_to_all x3 -> x0, blocking collectives: 824 us -> none  [the longest x2 634 us: device_step(): qkv_heads = lax.all_to_all(qkv_local, 'sp', 3, 1, tiled=True)]
    dot_general x12 -> x0, matrix products: 745 us -> none  [the longest x2 186 us: attend(): jnp.einsum('bqhe,bkhe->bhqk', q_part, k_part, preferred_element_type=jnp....]
    pallas_call x0 -> x1, Pallas kernels: none -> 555 us  [device_step(): pl.pallas_call(functools.partial(encoder_kernel, n, layers, heads, head_d...]
    all_to_all x6 -> x0, local copies, waits for them, and re-layouts: 196 us -> none  [the longest x4 123 us: device_step(): qkv_heads = lax.all_to_all(qkv_local, 'sp', 3, 1, tiled=True)]
    all_to_all x1 -> x0, waiting for transfers between devices: 181 us -> none  [device_step(): attn_tokens = lax.all_to_all(attn_heads, 'sp', 2, 1, tiled=True)]
    reduce_sum x7 -> x0, other arithmetic: 181 us -> none  [the longest x2 161 us: attend(): row_total = jnp.sum(prob_vals, axis=-1, keepdims=True)]
    convert_element_type x4 -> x0, local copies, waits for them, and re-layouts: 113 us -> none  [the longest x2 73.7 us: attend(): return (mixed_vals / row_total).astype(jnp.bfloat16)]
  transfers between devices with their start and end apart: 1 -> 0, of which waited for: 1 -> 0; matrix products, arithmetic and copies ran while one was open for 0% -> 0% of each run, Pallas kernels for 0% -> 0%
where the time goes in v2:
time: 575 us; the launch traced here: 574 us
  Pallas kernels  555 us (97%)
  local copies, waits for them, and re-layouts  19.3 us (3%)
    pallas_call x1, Pallas kernels, device_step(): pl.pallas_call(functools.partial(encoder_kernel, n, layers, heads, head_d...  555 us

profile of v2, /device:TPU:0, one launch (start us, length us, event | category | flops | bytes accessed | tf_op | source)
XLA Modules:
  0.0 574.1 jit_solution(9194740514164502660)
XLA Ops:
  0.0 1.3 reshape.30.g1_ref
  1.3 1.3 reshape.31.s1_ref
  2.6 1.3 reshape.35.bout_ref
  3.9 1.3 reshape.36.g2_ref
  5.2 1.3 reshape.37.s2_ref
  6.5 1.3 reshape.39.bdown_ref
  7.8 1.5 reshape.33.bqkv_ref
  9.3 1.4 reshape.38.bup_ref
  10.7 554.8 %encoder.1 = bf16[32,128,1152]{2,1,0:T(8,128)(2,1)} custom-call(bf16[32,128,1152]{2,1,0:T(8,128)(2,1)} %x_hbm.1, f32[2,1,1152]{2,1,0:T(1,128)} %reshape.30.g1_ref, f32[2,1,1152]{2,1,0:T(1,128)} %reshape.31.s1_ref, bf16[2,3456,1152]{2,1,0:T(8,128)(2,1)} %bitcast.8, f32[2,1,3456]{2,1,0:T(1,128)} %reshape.33.bqkv_ref, bf16[2,1152,1152]{2,1,0:T(8,128)(2,1)} %bitcast.9, ...), custom_call_target="tpu_custom_call" | custom-call | tf_op jit(solution)/shard_map/encoder/pallas_call | solution.py:241
  565.5 8.6 %copy.15 = bf16[32,128,1152]{2,1,0:T(8,128)(2,1)} copy(bf16[32,128,1152]{2,1,0:T(8,128)(2,1)} %encoder.1) | data formatting | bytes 18874368

commit v3 on v2

--- a/solution.py
+++ b/solution.py
@@ -14,6 +14,8 @@
 BF16, F32 = jnp.bfloat16, jnp.float32
 MESH = pl.DeviceIdType.MESH
 NT = (((1,), (1,)), ((), ()))
+RELATION = (0, 1, 2, 4, 3, 5, 6, 7)
+QKV_CHUNK, UP_CHUNK, DOWN_CHUNK = 512, 512, 1152
 
 
 def layer_norm(tokens, gain, shift):
@@ -44,7 +46,7 @@
     own, _, tile, width = h_ref.shape
     seq = n * tile
     mlp = wup_ref.shape[0]
-    rows = n_ref.shape[0]
+    rows = a_ref.shape[0]
     per = rows // tile
     tiles = n // per
     qb = s_ref.shape[2]
@@ -55,44 +57,46 @@
         src, dst = ((wqkv_hbm, wqkv_ref), (wout_hbm, wout_ref), (wup_hbm, wup_ref), (wdown_hbm, wdown_ref))[which]
         return pltpu.make_async_copy(src.at[layer], dst, w_sem.at[which])
 
-    def send_in(image, peer):
+    def peer_of(slot):
+        rel = RELATION[slot]
+        return sum((me // bit + rel // bit) % 2 * bit for bit in (1, 2, 4))
+
+    def send_in(image, slot):
+        peer = peer_of(slot)
         return pltpu.make_async_remote_copy(
-            src_ref=x_hbm.at[peer * own + image], dst_ref=h_ref.at[image, me],
-            send_sem=in_send.at[image, peer], recv_sem=in_recv.at[image, me], device_id=(dp, peer), device_id_type=MESH)
+            src_ref=x_hbm.at[peer * own + image], dst_ref=h_ref.at[image, slot],
+            send_sem=in_send.at[image, slot], recv_sem=in_recv.at[image, slot], device_id=(dp, peer), device_id_type=MESH)
 
     def keep_in(image):
-        return pltpu.make_async_copy(x_hbm.at[me * own + image], h_ref.at[image, me], in_recv.at[image, me])
-
-    def send_out(image, peer):
+        return pltpu.make_async_copy(x_hbm.at[me * own + image], h_ref.at[image, 0], in_recv.at[image, 0])
+
+    def send_out(image, slot):
         return pltpu.make_async_remote_copy(
-            src_ref=h_ref.at[image, peer], dst_ref=out_hbm.at[me * own + image],
-            send_sem=out_send.at[image, peer], recv_sem=out_recv.at[image, me], device_id=(dp, peer), device_id_type=MESH)
+            src_ref=h_ref.at[image, slot], dst_ref=out_hbm.at[me * own + image],
+            send_sem=out_send.at[image, slot], recv_sem=out_recv.at[image, slot], device_id=(dp, peer_of(slot)), device_id_type=MESH)
 
     def keep_out(image):
-        return pltpu.make_async_copy(h_ref.at[image, me], out_hbm.at[me * own + image], out_recv.at[image, me])
+        return pltpu.make_async_copy(h_ref.at[image, 0], out_hbm.at[me * own + image], out_recv.at[image, 0])
 
     for which in range(4):
         weight_copy(which, 0).start()
 
     barrier = pltpu.get_barrier_semaphore()
     for k in range(1, n):
-        pl.semaphore_signal(barrier, inc=1, device_id=(dp, lax.rem(me + k, n)), device_id_type=MESH)
+        pl.semaphore_signal(barrier, inc=1, device_id=(dp, peer_of(k)), device_id_type=MESH)
     pl.semaphore_wait(barrier, n - 1)
 
     def start_in(image, carry):
         keep_in(image).start()
-
-        def one(k, c):
-            send_in(image, lax.rem(me + k, n)).start()
-            return c
-
-        return lax.fori_loop(1, n, one, carry)
+        for slot in range(1, n):
+            send_in(image, slot).start()
+        return carry
 
     lax.fori_loop(0, own, start_in, 0)
 
     lanes = lax.broadcasted_iota(jnp.int32, (1, 256), 1)
+    scale = head_dim**-0.5 * LOG2E
     pair_rows = 2 * head_dim
-    scale = head_dim**-0.5 * LOG2E
     last_window = width // 128 - 2
     pairs = heads // 2
     units = [(hh, blk) for hh in range(2) for blk in range(seq // qb)]
@@ -111,7 +115,7 @@
         peak = jnp.max(s_ref[buf], axis=0, keepdims=True)
         total = jnp.zeros((1, qb), F32)
         for start, size in chunks(seq, 256):
-            prob = jnp.exp2((s_ref[buf, pl.ds(start, size), :] - peak) * scale)
+            prob = jnp.exp2(s_ref[buf, pl.ds(start, size), :] - peak)
             p_ref[buf, pl.ds(start, size), :] = prob.astype(BF16)
             total = total + jnp.sum(prob, axis=0, keepdims=True)
         lane0 = jnp.minimum(pair * pair_rows // 128, last_window) * 128
@@ -139,27 +143,49 @@
         def _():
             weight_copy(0, layer).wait()
 
-        @pl.when(layer == 0)
-        def _():
-            keep_in(image).wait()
-            for k in range(1, n):
-                src = lax.rem(me + n - k, n)
-                pltpu.make_async_remote_copy(
-                    src_ref=x_hbm.at[image], dst_ref=h_ref.at[image, src], send_sem=in_send.at[image, src],
-                    recv_sem=in_recv.at[image, src], device_id=(dp, src), device_id_type=MESH).wait_recv()
-
         def next_layer(which):
             @pl.when(jnp.logical_and(image == own - 1, layer < layers - 1))
             def _():
                 weight_copy(which, layer + 1).start()
 
+        def arrive(first, last):
+            @pl.when(layer == 0)
+            def _():
+                for slot in range(first, last):
+                    if slot:
+                        send_in(image, slot).wait_recv()
+                    else:
+                        keep_in(image).wait()
+
+        def row_of(ref, start, size):
+            return ref[pl.ds(layer, 1), :][:, start : start + size]
+
+        def qkv_columns(n_at, rows_at, start, size):
+            acc = lax.dot_general(n_ref[n_at, :], wqkv_ref[pl.ds(start, size), :], NT, preferred_element_type=F32)
+            acc = acc + row_of(bqkv_ref, start, size)
+            if start < width:
+                cols = start + lax.broadcasted_iota(jnp.int32, (1, size), 1)
+                acc = acc * jnp.where(cols < width, scale, 1.0)
+            qkv_ref[rows_at, pl.ds(start, size)] = acc.astype(BF16)
+
         def qkv_tile(t, c):
-            tokens = h_ref[image, pl.ds(t * per, per)].reshape(rows, width)
-            n_ref[...] = layer_norm(tokens, g1_ref[layer], s1_ref[layer])
-            at = pl.ds(pl.multiple_of(t * rows, rows), rows)
-            for start, size in chunks(3 * width, 512):
-                acc = lax.dot_general(n_ref[...], wqkv_ref[pl.ds(start, size), :], NT, preferred_element_type=F32)
-                qkv_ref[at, pl.ds(start, size)] = (acc + bqkv_ref[layer, :, pl.ds(start, size)]).astype(BF16)
+            @pl.when(layer == 0)
+            def _():
+                @pl.when(t == 0)
+                def _():
+                    arrive(0, per)
+
+                @pl.when(t == 1)
+                def _():
+                    arrive(per, n)
+
+            half = rows // 2
+            for sub in range(2):
+                tokens = h_ref[image, pl.ds(t * per + sub * per // 2, per // 2)].reshape(half, width)
+                n_ref[pl.ds(sub * half, half), :] = layer_norm(tokens, row_of(g1_ref, 0, width), row_of(s1_ref, 0, width))
+                qkv_columns(pl.ds(sub * half, half), pl.ds(pl.multiple_of(t * rows + sub * half, half), half), 0, 512)
+            for start, size in chunks(3 * width - 512, QKV_CHUNK):
+                qkv_columns(pl.ds(0, rows), pl.ds(pl.multiple_of(t * rows, rows), rows), 512 + start, size)
             return c
 
         lax.fori_loop(0, tiles, qkv_tile, 0)
@@ -172,36 +198,35 @@
             for which in range(1, 4):
                 weight_copy(which, layer).wait()
 
-        def mlp_tile(t, c):
+        def out_tile(t):
             blocks = pl.ds(t * per, per)
-            at = pl.ds(pl.multiple_of(t * rows, rows), rows)
-            acc = jnp.dot(ot_ref[:, at].T, wout_ref[...], preferred_element_type=F32) + bout_ref[layer]
+            acc = jnp.dot(ot_ref[:, pl.ds(t * rows, rows)].T, wout_ref[...], preferred_element_type=F32) + row_of(bout_ref, 0, width)
             mid = (h_ref[image, blocks].reshape(rows, width).astype(F32) + acc).astype(BF16)
             h_ref[image, blocks] = mid.reshape(per, tile, width)
-            n_ref[...] = layer_norm(mid, g2_ref[layer], s2_ref[layer])
-            for start, size in chunks(mlp, 512):
-                acc = lax.dot_general(n_ref[...], wup_ref[pl.ds(start, size), :], NT, preferred_element_type=F32)
-                a_ref[:, pl.ds(start, size)] = gelu_tanh(acc + bup_ref[layer, :, pl.ds(start, size)]).astype(BF16)
-            acc = jnp.dot(a_ref[...], wdown_ref[...], preferred_element_type=F32) + bdown_ref[layer]
-            new = h_ref[image, blocks].reshape(rows, width).astype(F32) + acc
-            h_ref[image, blocks] = new.astype(BF16).reshape(per, tile, width)
+            n_ref[pl.ds(t * rows, rows), :] = layer_norm(mid, row_of(g2_ref, 0, width), row_of(s2_ref, 0, width))
+
+        def mlp_tile(t):
+            blocks = pl.ds(t * per, per)
+            for start, size in chunks(mlp, UP_CHUNK):
+                acc = lax.dot_general(n_ref[pl.ds(t * rows, rows), :], wup_ref[pl.ds(start, size), :], NT, preferred_element_type=F32)
+                a_ref[:, pl.ds(start, size)] = gelu_tanh(acc + row_of(bup_ref, start, size)).astype(BF16)
+            for start, size in chunks(width, DOWN_CHUNK):
+                acc = jnp.dot(a_ref[...], wdown_ref[:, pl.ds(start, size)], preferred_element_type=F32) + row_of(bdown_ref, start, size)
+                new = h_ref[image, blocks, :, pl.ds(start, size)].reshape(rows, size).astype(F32) + acc
+                h_ref[image, blocks, :, pl.ds(start, size)] = new.astype(BF16).reshape(per, tile, size)
 
             @pl.when(layer == layers - 1)
             def _():
-                for part in range(per):
-                    peer = t * per + part
-
-                    @pl.when(peer == me)
-                    def _():
+                for slot in range(t * per, (t + 1) * per):
+                    if slot:
+                        send_out(image, slot).start()
+                    else:
                         keep_out(image).start()
 
-                    @pl.when(peer != me)
-                    def _():
-                        send_out(image, peer).start()
-
-            return c
-
-        lax.fori_loop(0, tiles, mlp_tile, 0)
+        for t in reversed(range(tiles)):
+            out_tile(t)
+        for t in reversed(range(tiles)):
+            mlp_tile(t)
         for which in range(1, 4):
             next_layer(which)
         return carry
@@ -210,13 +235,9 @@
 
     def drain(image, carry):
         keep_out(image).wait()
-        for k in range(1, n):
-            peer = lax.rem(me + k, n)
-            send_in(image, peer).wait_send()
-            send_out(image, peer).wait_send()
-            pltpu.make_async_remote_copy(
-                src_ref=h_ref.at[image, peer], dst_ref=out_hbm.at[peer * own + image], send_sem=out_send.at[image, peer],
-                recv_sem=out_recv.at[image, peer], device_id=(dp, peer), device_id_type=MESH).wait_recv()
+        for slot in range(1, n):
+            send_in(image, slot).wait_send()
+            send_out(image, slot).wait()
         return carry
 
     lax.fori_loop(0, own, drain, 0)
@@ -231,7 +252,6 @@
         layers, _, _, heads, head_dim = w_qkv.shape
         mlp = w_up.shape[2]
         own, seq = images // n, n * tile
-        row = lambda a: a.reshape(layers, 1, -1)
         w_qkv = jnp.swapaxes(w_qkv.reshape(layers, width, 3 * width), 1, 2)
         w_up = jnp.swapaxes(w_up, 1, 2)
         w_out = w_out.reshape(layers, width, width)
@@ -255,7 +275,7 @@
                 pltpu.VMEM((2 * head_dim, seq), F32),
                 pltpu.VMEM((2, seq, 256), F32),
                 pltpu.VMEM((2, seq, 256), BF16),
-                pltpu.VMEM((rows, width), BF16),
+                pltpu.VMEM((seq, width), BF16),
                 pltpu.VMEM((rows, mlp), BF16),
                 pltpu.SemaphoreType.DMA((4,)),
                 pltpu.SemaphoreType.DMA((own, n)),
@@ -266,8 +286,8 @@
             compiler_params=pltpu.CompilerParams(vmem_limit_bytes=VMEM_LIMIT, collective_id=0, has_side_effects=True),
             name='encoder',
         )(
-            image_tokens, row(ln1_gain), row(ln1_shift), w_qkv, row(b_qkv), w_out, row(b_out),
-            row(ln2_gain), row(ln2_shift), w_up, row(b_up), w_down, row(b_down),
+            image_tokens, ln1_gain, ln1_shift, w_qkv, b_qkv.reshape(layers, 3 * width), w_out, b_out,
+            ln2_gain, ln2_shift, w_up, b_up, w_down, b_down,
         )
 
     return jax.shard_map(device_step, mesh=mesh, in_specs=(token_spec,) + (P(),) * 12, out_specs=token_spec, check_vma=False)

time: 575 us -> 537 us (0.934)
  Pallas kernels: 555 us -> 527 us
  local copies, waits for them, and re-layouts: 19.3 us -> 10.1 us
    pallas_call x1, Pallas kernels: 555 us -> 527 us  [device_step(): pl.pallas_call(functools.partial(encoder_kernel, n, layers, heads, head_d...]
    reshape x8 -> x1, local copies, waits for them, and re-layouts: 10.7 us -> 1.51 us  [device_step(): b_qkv.reshape(layers, 3 * width)]
where the time goes in v3:
time: 537 us
  Pallas kernels  527 us (98%)
  local copies, waits for them, and re-layouts  10.1 us (2%)
    pallas_call x1, Pallas kernels, device_step(): pl.pallas_call(functools.partial(encoder_kernel, n, layers, heads, head_d...  527 us

profile of v3, /device:TPU:0, one launch (start us, length us, event | category | flops | bytes accessed | tf_op | source)
XLA Modules:
  0.0 537.2 jit_solution(7855915327381995694)
XLA Ops:
  0.0 1.5 reshape.10.bqkv_ref
  1.5 527.0 %encoder.1 = bf16[32,128,1152]{2,1,0:T(8,128)(2,1)} custom-call(bf16[32,128,1152]{2,1,0:T(8,128)(2,1)} %x_hbm.1, f32[2,1152]{1,0:T(2,128)} %g1_ref.1, f32[2,1152]{1,0:T(2,128)} %s1_ref.1, bf16[2,3456,1152]{2,1,0:T(8,128)(2,1)} %bitcast.8, f32[2,3456]{1,0:T(2,128)} %reshape.10.bqkv_ref, bf16[2,1152,1152]{2,1,0:T(8,128)(2,1)} %bitcast.9, f32[2,1152]{1,0:T(2,128)} %bout_ref.1, ...), custom_call_target="tpu_custom_call" | custom-call | tf_op jit(solution)/shard_map/encoder/pallas_call | solution.py:261
  528.6 8.6 %copy.15 = bf16[32,128,1152]{2,1,0:T(8,128)(2,1)} copy(bf16[32,128,1152]{2,1,0:T(8,128)(2,1)} %encoder.1) | data formatting | bytes 18874368

commit v4 on v3

--- a/solution.py
+++ b/solution.py
@@ -16,6 +16,7 @@
 NT = (((1,), (1,)), ((), ()))
 RELATION = (0, 1, 2, 4, 3, 5, 6, 7)
 QKV_CHUNK, UP_CHUNK, DOWN_CHUNK = 512, 512, 1152
+PAIRS, BUFFERS, AHEAD = 1, 4, 2
 
 
 def layer_norm(tokens, gain, shift):
@@ -36,17 +37,26 @@
     return [(start, min(step, total - start)) for start in range(0, total, step)]
 
 
+def to_planes(ref, start, rows_at, values):
+    for lane, size in chunks(values.shape[1], 128):
+        ref[(start + lane) // 128, rows_at, pl.ds(0, size)] = values[:, lane : lane + size]
+
+
+def from_planes(ref, rows_at, total):
+    return jnp.concatenate([ref[start // 128, rows_at, pl.ds(0, size)] for start, size in chunks(total, 128)], axis=1)
+
+
 def encoder_kernel(
     n, layers, heads, head_dim,
     x_hbm, g1_ref, s1_ref, wqkv_hbm, bqkv_ref, wout_hbm, bout_ref, g2_ref, s2_ref, wup_hbm, bup_ref, wdown_hbm, bdown_ref,
     out_hbm,
-    h_ref, wqkv_ref, wout_ref, wup_ref, wdown_ref, qkv_ref, vt_ref, ot_ref, of_ref, s_ref, p_ref, n_ref, a_ref,
+    h_ref, wqkv_ref, wout_ref, wup_ref, wdown_ref, qkv_ref, vt_ref, ot_ref, of_ref, s_ref, a_ref,
     w_sem, in_send, in_recv, out_send, out_recv,
 ):
     own, _, tile, width = h_ref.shape
     seq = n * tile
     mlp = wup_ref.shape[0]
-    rows = a_ref.shape[0]
+    rows = a_ref.shape[1]
     per = rows // tile
     tiles = n // per
     qb = s_ref.shape[2]
@@ -99,41 +109,54 @@
     pair_rows = 2 * head_dim
     last_window = width // 128 - 2
     pairs = heads // 2
-    units = [(hh, blk) for hh in range(2) for blk in range(seq // qb)]
+    planes = width // 128
+
+    def window(first):
+        return jnp.minimum(first // 128, last_window)
+
+    def two_planes(plane, start, size):
+        return jnp.concatenate([qkv_ref[plane + i, pl.ds(start, size), :] for i in range(2)], axis=1)
 
     def scores(pair, hh, blk, buf):
         first = (pair * 2 + hh) * head_dim
-        off = pl.multiple_of(jnp.minimum(first // 128, last_window) * 128, 128)
-        mask = jnp.logical_and(lanes + off >= first, lanes + off < first + head_dim)
-        q_win = qkv_ref[pl.ds(blk * qb, qb), pl.ds(off, 256)]
+        plane = window(first)
+        mask = jnp.logical_and(lanes + plane * 128 >= first, lanes + plane * 128 < first + head_dim)
+        q_win = two_planes(plane, blk * qb, qb)
         q_win = jnp.where(mask, q_win, jnp.zeros_like(q_win))
         for half in range(2):
-            k_win = qkv_ref[pl.ds(half * (seq // 2), seq // 2), pl.ds(width + off, 256)]
+            k_win = two_planes(planes + plane, half * (seq // 2), seq // 2)
             s_ref[buf, pl.ds(half * (seq // 2), seq // 2), :] = lax.dot_general(k_win, q_win, NT, preferred_element_type=F32)
 
-    def finish(pair, hh, blk, buf):
+    def finish(pair, e, hh, blk, buf):
         peak = jnp.max(s_ref[buf], axis=0, keepdims=True)
         total = jnp.zeros((1, qb), F32)
+        probs = []
         for start, size in chunks(seq, 256):
             prob = jnp.exp2(s_ref[buf, pl.ds(start, size), :] - peak)
-            p_ref[buf, pl.ds(start, size), :] = prob.astype(BF16)
+            probs.append(prob.astype(BF16))
             total = total + jnp.sum(prob, axis=0, keepdims=True)
-        lane0 = jnp.minimum(pair * pair_rows // 128, last_window) * 128
-        v_rows = pl.multiple_of(pair * pair_rows - lane0 + 64 * hh, 16)
-        mixed = jnp.dot(vt_ref[pl.ds(v_rows, 80), :], p_ref[buf], preferred_element_type=F32)
-        of_ref[pl.ds(hh * head_dim, head_dim), pl.ds(blk * qb, qb)] = mixed[8 * hh : 8 * hh + head_dim] * (1.0 / total)
-
-    def pair_body(pair, carry):
-        lane0 = pl.multiple_of(jnp.minimum(pair * pair_rows // 128, last_window) * 128, 128)
-        vt_ref[...] = qkv_ref[:, pl.ds(2 * width + lane0, 256)].T
-        following = jnp.minimum(pair + 1, pairs - 1)
-        for i, (hh, blk) in enumerate(units):
-            if i + 1 < len(units):
-                scores(pair, *units[i + 1], (i + 1) % 2)
-            else:
-                scores(following, *units[0], (i + 1) % 2)
-            finish(pair, hh, blk, i % 2)
-        ot_ref[pl.ds(pl.multiple_of(pair * pair_rows, 16), pair_rows), :] = of_ref[...].astype(BF16)
+        first = pair * pair_rows
+        v_rows = pl.multiple_of(first - window(first) * 128 + 64 * hh, 16)
+        values = jnp.concatenate([vt_ref[e, part, pl.ds(v_rows, 80), :] for part in range(seq // 128)], axis=1)
+        mixed = jnp.dot(values, jnp.concatenate(probs, axis=0), preferred_element_type=F32)
+        of_ref[e, pl.ds(hh * head_dim, head_dim), pl.ds(blk * qb, qb)] = mixed[8 * hh : 8 * hh + head_dim] * (1.0 / total)
+
+    units = [(e, hh, blk) for e in range(PAIRS) for hh in range(2) for blk in range(seq // qb)]
+
+    def pairs_body(it, carry):
+        following = jnp.minimum((it + 1) * PAIRS, pairs - 1)
+        for e in range(PAIRS):
+            plane = 2 * planes + window((it * PAIRS + e) * pair_rows)
+            for part in range(seq // 128):
+                vt_ref[e, part] = two_planes(plane, part * 128, 128).T
+        for i, (e, hh, blk) in enumerate(units):
+            ahead = i + AHEAD
+            e1, hh1, blk1 = units[ahead % len(units)]
+            scores(it * PAIRS + e1 if ahead < len(units) else following, hh1, blk1, ahead % BUFFERS)
+            finish(it * PAIRS + e, e, hh, blk, i % BUFFERS)
+            if (hh, blk) == (1, seq // qb - 1):
+                at = pl.multiple_of((it * PAIRS + e) * pair_rows, 16)
+                ot_ref[pl.ds(at, pair_rows), :] = of_ref[e].astype(BF16)
         return carry
 
     def step(g, carry):
@@ -161,12 +184,12 @@
             return ref[pl.ds(layer, 1), :][:, start : start + size]
 
         def qkv_columns(n_at, rows_at, start, size):
-            acc = lax.dot_general(n_ref[n_at, :], wqkv_ref[pl.ds(start, size), :], NT, preferred_element_type=F32)
+            acc = lax.dot_general(from_planes(a_ref, n_at, width), wqkv_ref[pl.ds(start, size), :], NT, preferred_element_type=F32)
             acc = acc + row_of(bqkv_ref, start, size)
             if start < width:
                 cols = start + lax.broadcasted_iota(jnp.int32, (1, size), 1)
                 acc = acc * jnp.where(cols < width, scale, 1.0)
-            qkv_ref[rows_at, pl.ds(start, size)] = acc.astype(BF16)
+            to_planes(qkv_ref, start, rows_at, acc.astype(BF16))
 
         def qkv_tile(t, c):
             @pl.when(layer == 0)
@@ -182,7 +205,8 @@
             half = rows // 2
             for sub in range(2):
                 tokens = h_ref[image, pl.ds(t * per + sub * per // 2, per // 2)].reshape(half, width)
-                n_ref[pl.ds(sub * half, half), :] = layer_norm(tokens, row_of(g1_ref, 0, width), row_of(s1_ref, 0, width))
+                normed = layer_norm(tokens, row_of(g1_ref, 0, width), row_of(s1_ref, 0, width))
+                to_planes(a_ref, 0, pl.ds(sub * half, half), normed)
                 qkv_columns(pl.ds(sub * half, half), pl.ds(pl.multiple_of(t * rows + sub * half, half), half), 0, 512)
             for start, size in chunks(3 * width - 512, QKV_CHUNK):
                 qkv_columns(pl.ds(0, rows), pl.ds(pl.multiple_of(t * rows, rows), rows), 512 + start, size)
@@ -190,8 +214,9 @@
 
         lax.fori_loop(0, tiles, qkv_tile, 0)
         next_layer(0)
-        scores(0, *units[0], 0)
-        lax.fori_loop(0, pairs, pair_body, 0)
+        for i, (_, hh, blk) in enumerate(units[:AHEAD]):
+            scores(0, hh, blk, i)
+        lax.fori_loop(0, pairs // PAIRS, pairs_body, 0)
 
         @pl.when(image == 0)
         def _():
@@ -203,15 +228,15 @@
             acc = jnp.dot(ot_ref[:, pl.ds(t * rows, rows)].T, wout_ref[...], preferred_element_type=F32) + row_of(bout_ref, 0, width)
             mid = (h_ref[image, blocks].reshape(rows, width).astype(F32) + acc).astype(BF16)
             h_ref[image, blocks] = mid.reshape(per, tile, width)
-            n_ref[pl.ds(t * rows, rows), :] = layer_norm(mid, row_of(g2_ref, 0, width), row_of(s2_ref, 0, width))
+            to_planes(qkv_ref, 0, pl.ds(t * rows, rows), layer_norm(mid, row_of(g2_ref, 0, width), row_of(s2_ref, 0, width)))
 
         def mlp_tile(t):
             blocks = pl.ds(t * per, per)
             for start, size in chunks(mlp, UP_CHUNK):
-                acc = lax.dot_general(n_ref[pl.ds(t * rows, rows), :], wup_ref[pl.ds(start, size), :], NT, preferred_element_type=F32)
-                a_ref[:, pl.ds(start, size)] = gelu_tanh(acc + row_of(bup_ref, start, size)).astype(BF16)
+                acc = lax.dot_general(from_planes(qkv_ref, pl.ds(t * rows, rows), width), wup_ref[pl.ds(start, size), :], NT, preferred_element_type=F32)
+                to_planes(a_ref, start, pl.ds(0, rows), gelu_tanh(acc + row_of(bup_ref, start, size)).astype(BF16))
             for start, size in chunks(width, DOWN_CHUNK):
-                acc = jnp.dot(a_ref[...], wdown_ref[:, pl.ds(start, size)], preferred_element_type=F32) + row_of(bdown_ref, start, size)
+                acc = jnp.dot(from_planes(a_ref, pl.ds(0, rows), mlp), wdown_ref[:, pl.ds(start, size)], preferred_element_type=F32) + row_of(bdown_ref, start, size)
                 new = h_ref[image, blocks, :, pl.ds(start, size)].reshape(rows, size).astype(F32) + acc
                 h_ref[image, blocks, :, pl.ds(start, size)] = new.astype(BF16).reshape(per, tile, size)
 
@@ -269,14 +294,12 @@
                 pltpu.VMEM((width, width), BF16),
                 pltpu.VMEM((mlp, width), BF16),
                 pltpu.VMEM((mlp, width), BF16),
-                pltpu.VMEM((seq, 3 * width), BF16),
-                pltpu.VMEM((256, seq), BF16),
+                pltpu.VMEM((3 * width // 128, seq, 128), BF16),
+                pltpu.VMEM((PAIRS, seq // 128, 256, 128), BF16),
                 pltpu.VMEM((width, seq), BF16),
-                pltpu.VMEM((2 * head_dim, seq), F32),
-                pltpu.VMEM((2, seq, 256), F32),
-                pltpu.VMEM((2, seq, 256), BF16),
-                pltpu.VMEM((seq, width), BF16),
-                pltpu.VMEM((rows, mlp), BF16),
+                pltpu.VMEM((PAIRS, 2 * head_dim, seq), F32),
+                pltpu.VMEM((BUFFERS, seq, 256), F32),
+                pltpu.VMEM((pl.cdiv(mlp, 128), rows, 128), BF16),
                 pltpu.SemaphoreType.DMA((4,)),
                 pltpu.SemaphoreType.DMA((own, n)),
                 pltpu.SemaphoreType.DMA((own, n)),

time: 537 us -> 536 us (level)
  no operation moved by 1% of the time
where the time goes in v4:
time: 536 us
  Pallas kernels  526 us (98%)
  local copies, waits for them, and re-layouts  10.1 us (2%)
    pallas_call x1, Pallas kernels, device_step(): pl.pallas_call(functools.partial(encoder_kernel, n, layers, heads, head_d...  526 us

profile of v4, /device:TPU:0, one launch (start us, length us, event | category | flops | bytes accessed | tf_op | source)
XLA Modules:
  0.0 535.9 jit_solution(1127845770376479994)
XLA Ops:
  0.0 1.5 reshape.10.bqkv_ref
  1.5 525.8 %encoder.1 = bf16[32,128,1152]{2,1,0:T(8,128)(2,1)} custom-call(bf16[32,128,1152]{2,1,0:T(8,128)(2,1)} %x_hbm.1, f32[2,1152]{1,0:T(2,128)} %g1_ref.1, f32[2,1152]{1,0:T(2,128)} %s1_ref.1, bf16[2,3456,1152]{2,1,0:T(8,128)(2,1)} %bitcast.8, f32[2,3456]{1,0:T(2,128)} %reshape.10.bqkv_ref, bf16[2,1152,1152]{2,1,0:T(8,128)(2,1)} %bitcast.9, f32[2,1152]{1,0:T(2,128)} %bout_ref.1, ...), custom_call_target="tpu_custom_call" | custom-call | tf_op jit(solution)/shard_map/encoder/pallas_call | solution.py:286
  527.4 8.6 %copy.15 = bf16[32,128,1152]{2,1,0:T(8,128)(2,1)} copy(bf16[32,128,1152]{2,1,0:T(8,128)(2,1)} %encoder.1) | data formatting | bytes 18874368

commit v5 on v4

--- a/solution.py
+++ b/solution.py
@@ -16,7 +16,7 @@
 NT = (((1,), (1,)), ((), ()))
 RELATION = (0, 1, 2, 4, 3, 5, 6, 7)
 QKV_CHUNK, UP_CHUNK, DOWN_CHUNK = 512, 512, 1152
-PAIRS, BUFFERS, AHEAD = 1, 4, 2
+PAIRS, BUFFERS, AHEAD = 2, 4, 2
 
 
 def layer_norm(tokens, gain, shift):
@@ -50,7 +50,7 @@
     n, layers, heads, head_dim,
     x_hbm, g1_ref, s1_ref, wqkv_hbm, bqkv_ref, wout_hbm, bout_ref, g2_ref, s2_ref, wup_hbm, bup_ref, wdown_hbm, bdown_ref,
     out_hbm,
-    h_ref, wqkv_ref, wout_ref, wup_ref, wdown_ref, qkv_ref, vt_ref, ot_ref, of_ref, s_ref, a_ref,
+    h_ref, wqkv_ref, wout_ref, wup_ref, wdown_ref, qk_ref, vt_ref, ot_ref, of_ref, s_ref, a_ref,
     w_sem, in_send, in_recv, out_send, out_recv,
 ):
     own, _, tile, width = h_ref.shape
@@ -115,7 +115,7 @@
         return jnp.minimum(first // 128, last_window)
 
     def two_planes(plane, start, size):
-        return jnp.concatenate([qkv_ref[plane + i, pl.ds(start, size), :] for i in range(2)], axis=1)
+        return jnp.concatenate([qk_ref[plane + i, pl.ds(start, size), :] for i in range(2)], axis=1)
 
     def scores(pair, hh, blk, buf):
         first = (pair * 2 + hh) * head_dim
@@ -127,7 +127,7 @@
             k_win = two_planes(planes + plane, half * (seq // 2), seq // 2)
             s_ref[buf, pl.ds(half * (seq // 2), seq // 2), :] = lax.dot_general(k_win, q_win, NT, preferred_element_type=F32)
 
-    def finish(pair, e, hh, blk, buf):
+    def softmax(buf):
         peak = jnp.max(s_ref[buf], axis=0, keepdims=True)
         total = jnp.zeros((1, qb), F32)
         probs = []
@@ -135,28 +135,31 @@
             prob = jnp.exp2(s_ref[buf, pl.ds(start, size), :] - peak)
             probs.append(prob.astype(BF16))
             total = total + jnp.sum(prob, axis=0, keepdims=True)
-        first = pair * pair_rows
-        v_rows = pl.multiple_of(first - window(first) * 128 + 64 * hh, 16)
-        values = jnp.concatenate([vt_ref[e, part, pl.ds(v_rows, 80), :] for part in range(seq // 128)], axis=1)
-        mixed = jnp.dot(values, jnp.concatenate(probs, axis=0), preferred_element_type=F32)
+        return jnp.concatenate(probs, axis=0), total
+
+    def mix(pair, e, hh, blk, probs, total):
+        v_rows = pl.ds(pl.multiple_of(pair * pair_rows + 64 * hh, 16), 80)
+        values = jnp.concatenate([vt_ref[part, v_rows, :] for part in range(seq // 128)], axis=1)
+        mixed = jnp.dot(values, probs, preferred_element_type=F32)
         of_ref[e, pl.ds(hh * head_dim, head_dim), pl.ds(blk * qb, qb)] = mixed[8 * hh : 8 * hh + head_dim] * (1.0 / total)
 
     units = [(e, hh, blk) for e in range(PAIRS) for hh in range(2) for blk in range(seq // qb)]
 
     def pairs_body(it, carry):
         following = jnp.minimum((it + 1) * PAIRS, pairs - 1)
-        for e in range(PAIRS):
-            plane = 2 * planes + window((it * PAIRS + e) * pair_rows)
-            for part in range(seq // 128):
-                vt_ref[e, part] = two_planes(plane, part * 128, 128).T
+        waiting = None
         for i, (e, hh, blk) in enumerate(units):
             ahead = i + AHEAD
             e1, hh1, blk1 = units[ahead % len(units)]
             scores(it * PAIRS + e1 if ahead < len(units) else following, hh1, blk1, ahead % BUFFERS)
-            finish(it * PAIRS + e, e, hh, blk, i % BUFFERS)
-            if (hh, blk) == (1, seq // qb - 1):
-                at = pl.multiple_of((it * PAIRS + e) * pair_rows, 16)
-                ot_ref[pl.ds(at, pair_rows), :] = of_ref[e].astype(BF16)
+            done = softmax(i % BUFFERS)
+            if waiting:
+                mix(*waiting)
+            waiting = (it * PAIRS + e, e, hh, blk, *done)
+        mix(*waiting)
+        for e in range(PAIRS):
+            at = pl.multiple_of((it * PAIRS + e) * pair_rows, 16)
+            ot_ref[pl.ds(at, pair_rows), :] = of_ref[e].astype(BF16)
         return carry
 
     def step(g, carry):
@@ -183,13 +186,20 @@
         def row_of(ref, start, size):
             return ref[pl.ds(layer, 1), :][:, start : start + size]
 
-        def qkv_columns(n_at, rows_at, start, size):
+        def qk_columns(n_at, rows_at, start, size):
             acc = lax.dot_general(from_planes(a_ref, n_at, width), wqkv_ref[pl.ds(start, size), :], NT, preferred_element_type=F32)
             acc = acc + row_of(bqkv_ref, start, size)
             if start < width:
                 cols = start + lax.broadcasted_iota(jnp.int32, (1, size), 1)
                 acc = acc * jnp.where(cols < width, scale, 1.0)
-            to_planes(qkv_ref, start, rows_at, acc.astype(BF16))
+            to_planes(qk_ref, start, rows_at, acc.astype(BF16))
+
+        def v_columns(t, start, size):
+            first = 2 * width + start
+            acc = lax.dot_general(from_planes(a_ref, pl.ds(0, rows), width), wqkv_ref[pl.ds(first, size), :], NT, preferred_element_type=F32)
+            flipped = (acc + row_of(bqkv_ref, first, size)).astype(BF16).T
+            for part in range(per):
+                vt_ref[t * per + part, pl.ds(start, size), :] = flipped[:, part * tile : (part + 1) * tile]
 
         def qkv_tile(t, c):
             @pl.when(layer == 0)
@@ -207,9 +217,11 @@
                 tokens = h_ref[image, pl.ds(t * per + sub * per // 2, per // 2)].reshape(half, width)
                 normed = layer_norm(tokens, row_of(g1_ref, 0, width), row_of(s1_ref, 0, width))
                 to_planes(a_ref, 0, pl.ds(sub * half, half), normed)
-                qkv_columns(pl.ds(sub * half, half), pl.ds(pl.multiple_of(t * rows + sub * half, half), half), 0, 512)
-            for start, size in chunks(3 * width - 512, QKV_CHUNK):
-                qkv_columns(pl.ds(0, rows), pl.ds(pl.multiple_of(t * rows, rows), rows), 512 + start, size)
+                qk_columns(pl.ds(sub * half, half), pl.ds(pl.multiple_of(t * rows + sub * half, half), half), 0, 512)
+            for start, size in chunks(width, QKV_CHUNK):
+                v_columns(t, start, size)
+            for start, size in chunks(2 * width - 512, QKV_CHUNK):
+                qk_columns(pl.ds(0, rows), pl.ds(pl.multiple_of(t * rows, rows), rows), 512 + start, size)
             return c
 
         lax.fori_loop(0, tiles, qkv_tile, 0)
@@ -228,12 +240,12 @@
             acc = jnp.dot(ot_ref[:, pl.ds(t * rows, rows)].T, wout_ref[...], preferred_element_type=F32) + row_of(bout_ref, 0, width)
             mid = (h_ref[image, blocks].reshape(rows, width).astype(F32) + acc).astype(BF16)
             h_ref[image, blocks] = mid.reshape(per, tile, width)
-            to_planes(qkv_ref, 0, pl.ds(t * rows, rows), layer_norm(mid, row_of(g2_ref, 0, width), row_of(s2_ref, 0, width)))
+            to_planes(qk_ref, 0, pl.ds(t * rows, rows), layer_norm(mid, row_of(g2_ref, 0, width), row_of(s2_ref, 0, width)))
 
         def mlp_tile(t):
             blocks = pl.ds(t * per, per)
             for start, size in chunks(mlp, UP_CHUNK):
-                acc = lax.dot_general(from_planes(qkv_ref, pl.ds(t * rows, rows), width), wup_ref[pl.ds(start, size), :], NT, preferred_element_type=F32)
+                acc = lax.dot_general(from_planes(qk_ref, pl.ds(t * rows, rows), width), wup_ref[pl.ds(start, size), :], NT, preferred_element_type=F32)
                 to_planes(a_ref, start, pl.ds(0, rows), gelu_tanh(acc + row_of(bup_ref, start, size)).astype(BF16))
             for start, size in chunks(width, DOWN_CHUNK):
                 acc = jnp.dot(from_planes(a_ref, pl.ds(0, rows), mlp), wdown_ref[:, pl.ds(start, size)], preferred_element_type=F32) + row_of(bdown_ref, start, size)
@@ -294,8 +306,8 @@
                 pltpu.VMEM((width, width), BF16),
                 pltpu.VMEM((mlp, width), BF16),
                 pltpu.VMEM((mlp, width), BF16),
-                pltpu.VMEM((3 * width // 128, seq, 128), BF16),
-                pltpu.VMEM((PAIRS, seq // 128, 256, 128), BF16),
+                pltpu.VMEM((2 * width // 128, seq, 128), BF16),
+                pltpu.VMEM((seq // 128, width, 128), BF16),
                 pltpu.VMEM((width, seq), BF16),
                 pltpu.VMEM((PAIRS, 2 * head_dim, seq), F32),
                 pltpu.VMEM((BUFFERS, seq, 256), F32),

time: 536 us -> 526 us (0.981)
  Pallas kernels: 526 us -> 516 us
    pallas_call x1, Pallas kernels: 526 us -> 516 us  [device_step(): pl.pallas_call(functools.partial(encoder_kernel, n, layers, heads, head_d...]
where the time goes in v5:
time: 526 us
  Pallas kernels  516 us (98%)
  local copies, waits for them, and re-layouts  10.1 us (2%)
    pallas_call x1, Pallas kernels, device_step(): pl.pallas_call(functools.partial(encoder_kernel, n, layers, heads, head_d...  516 us

profile of v5, /device:TPU:0, one launch (start us, length us, event | category | flops | bytes accessed | tf_op | source)
XLA Modules:
  0.0 525.6 jit_solution(4268221833946700794)
XLA Ops:
  0.0 1.5 reshape.10.bqkv_ref
  1.5 515.5 %encoder.1 = bf16[32,128,1152]{2,1,0:T(8,128)(2,1)} custom-call(bf16[32,128,1152]{2,1,0:T(8,128)(2,1)} %x_hbm.1, f32[2,1152]{1,0:T(2,128)} %g1_ref.1, f32[2,1152]{1,0:T(2,128)} %s1_ref.1, bf16[2,3456,1152]{2,1,0:T(8,128)(2,1)} %bitcast.8, f32[2,3456]{1,0:T(2,128)} %reshape.10.bqkv_ref, bf16[2,1152,1152]{2,1,0:T(8,128)(2,1)} %bitcast.9, f32[2,1152]{1,0:T(2,128)} %bout_ref.1, ...), custom_call_target="tpu_custom_call" | custom-call | tf_op jit(solution)/shard_map/encoder/pallas_call | solution.py:298
  517.0 8.6 %copy.15 = bf16[32,128,1152]{2,1,0:T(8,128)(2,1)} copy(bf16[32,128,1152]{2,1,0:T(8,128)(2,1)} %encoder.1) | data formatting | bytes 18874368
